TPU v7x, 64 devices: a 2x2x8 block of a 4x4x8 slice. The times are simulated.
64 devices in a mesh: dp: 4 (over x, y), cp: 16 (over z, core).
Axes of the slice: x: 2, y: 2, z: 8, core: 2. Of those that a mesh axis runs over, the one named last changes fastest.
The devices are a block of a 4x4x8 slice.
Arguments:
- hidden: bfloat16 [32768, 4096], P(('dp', 'cp')), parts along dimension 0
- grad_out: bfloat16 [32768, 4096], P(('dp', 'cp')), parts along dimension 0
- w_query: bfloat16 [4096, 4, 128], replicated
- w_key: bfloat16 [4096, 1, 128], replicated
- w_value: bfloat16 [4096, 1, 128], replicated
- w_out: bfloat16 [4, 128, 4096], replicated
Outputs:
- output 1: bfloat16 [32768, 4096], P(('dp', 'cp')), parts along dimension 0
- output 2: bfloat16 [32768, 4096], P(('dp', 'cp')), parts along dimension 0
- output 3: float32 [16384, 4, 128], P('dp'), parts along dimension 0
- output 4: float32 [16384, 1, 128], P('dp'), parts along dimension 0
- output 5: float32 [16384, 1, 128], P('dp'), parts along dimension 0
- output 6: float32 [16, 128, 4096], P('dp'), parts along dimension 0
There are 4 independent parts. A program takes and returns all parts, laid end to end along the dimension named above; an argument that names none is the same for every part.
All inputs are finite; a program needn't handle non-finite values.
Results may differ from a plain program's by a relative error of at most 0.010751.
Values are sent between devices in bfloat16 or wider.
A program may use at most 768 MiB of HBM per device.

v0:
```python
import jax
import jax.numpy as jnp
from jax import lax
from jax.sharding import PartitionSpec as P


def token_positions(groups, tok_local):
    half_len = tok_local // 2
    row_ids = jnp.arange(groups * tok_local)
    owner_dev = row_ids // tok_local
    within = row_ids % tok_local
    block_idx = jnp.where(within < half_len, owner_dev, 2 * groups - 1 - owner_dev)
    return block_idx * half_len + within % half_len


def solution(mesh):
    groups = mesh.shape["cp"]
    row_spec = P(("dp", "cp"), None)
    rep_spec = P(None, None, None)
    part_spec = P("dp", None, None)

    def device_layer(hidden, grad_out, w_query, w_key, w_value, w_out):
        tok_local, model_width = hidden.shape
        num_heads, head_dim = w_query.shape[1], w_query.shape[2]
        kv_heads = w_key.shape[1]
        group_size = num_heads // kv_heads
        half_len = tok_local // 2
        score_scale = head_dim ** -0.5
        group_rank = lax.axis_index("cp")
        key_pos = token_positions(groups, tok_local)
        local_idx = jnp.arange(tok_local)
        query_pos = jnp.where(local_idx < half_len, group_rank, 2 * groups - 1 - group_rank) * half_len + local_idx % half_len
        visible = query_pos[:, None] >= key_pos[None, :]
        wq_flat = w_query.reshape(model_width, num_heads * head_dim)
        wk_flat = w_key.reshape(model_width, kv_heads * head_dim)
        wv_flat = w_value.reshape(model_width, kv_heads * head_dim)
        wo_flat = w_out.reshape(num_heads * head_dim, model_width)
        query_heads = jnp.dot(hidden, wq_flat, preferred_element_type=jnp.float32).astype(jnp.bfloat16)
        query_heads = query_heads.reshape(tok_local, kv_heads, group_size, head_dim)
        key_local = jnp.dot(hidden, wk_flat, preferred_element_type=jnp.float32).astype(jnp.bfloat16)
        value_local = jnp.dot(hidden, wv_flat, preferred_element_type=jnp.float32).astype(jnp.bfloat16)
        kv_local = jnp.stack([key_local, value_local]).reshape(2, tok_local, kv_heads, head_dim)
        kv_all = lax.all_gather(kv_local, "cp", axis=1, tiled=True)
        key_rows, value_rows = kv_all[0], kv_all[1]
        scores = jnp.einsum("tkgd,skd->kgts", query_heads, key_rows, preferred_element_type=jnp.float32) * score_scale
        masked = jnp.where(visible, scores, -jnp.inf)
        log_norm = jax.nn.logsumexp(masked, axis=-1)
        att_probs = jnp.exp(masked - log_norm[..., None]).astype(jnp.bfloat16)
        attended = jnp.einsum("kgts,skd->tkgd", att_probs, value_rows, preferred_element_type=jnp.float32).astype(jnp.bfloat16)
        att_flat = attended.reshape(tok_local, num_heads * head_dim)
        output = jnp.dot(att_flat, wo_flat, preferred_element_type=jnp.float32).astype(jnp.bfloat16)
        dout_flat = jnp.einsum("tm,em->te", grad_out, wo_flat, preferred_element_type=jnp.float32).astype(jnp.bfloat16)
        dout_heads = dout_flat.reshape(tok_local, kv_heads, group_size, head_dim)
        delta_rows = jnp.einsum("tkgd,tkgd->kgt", dout_heads, attended, preferred_element_type=jnp.float32)
        d_probs = jnp.einsum("tkgd,skd->kgts", dout_heads, value_rows, preferred_element_type=jnp.float32)
        d_scores = (att_probs.astype(jnp.float32) * (d_probs - delta_rows[..., None])).astype(jnp.bfloat16)
        query_grad = jnp.einsum("kgts,skd->tkgd", d_scores, key_rows, preferred_element_type=jnp.float32) * score_scale
        query_grad = query_grad.astype(jnp.bfloat16).reshape(tok_local, num_heads * head_dim)
        key_part = jnp.einsum("kgts,tkgd->skd", d_scores, query_heads, preferred_element_type=jnp.float32) * score_scale
        value_part = jnp.einsum("kgts,tkgd->skd", att_probs, dout_heads, preferred_element_type=jnp.float32)
        kv_grad = lax.psum_scatter(jnp.stack([key_part, value_part]), "cp", scatter_dimension=1, tiled=True)
        key_grad = kv_grad[0].astype(jnp.bfloat16).reshape(tok_local, kv_heads * head_dim)
        value_grad = kv_grad[1].astype(jnp.bfloat16).reshape(tok_local, kv_heads * head_dim)
        grad_hidden = (
            jnp.einsum("te,me->tm", query_grad, wq_flat, preferred_element_type=jnp.float32)
            + jnp.einsum("te,me->tm", key_grad, wk_flat, preferred_element_type=jnp.float32)
            + jnp.einsum("te,me->tm", value_grad, wv_flat, preferred_element_type=jnp.float32)
        ).astype(jnp.bfloat16)
        weight_parts = (
            jnp.einsum("tm,te->me", hidden, query_grad, preferred_element_type=jnp.float32),
            jnp.einsum("tm,te->me", hidden, key_grad, preferred_element_type=jnp.float32),
            jnp.einsum("tm,te->me", hidden, value_grad, preferred_element_type=jnp.float32),
            jnp.einsum("te,tm->em", att_flat, grad_out, preferred_element_type=jnp.float32),
        )
        grad_w_query, grad_w_key, grad_w_value, grad_w_out = lax.psum(weight_parts, "cp")
        return (
            output,
            grad_hidden,
            grad_w_query.reshape(model_width, num_heads, head_dim),
            grad_w_key.reshape(model_width, kv_heads, head_dim),
            grad_w_value.reshape(model_width, kv_heads, head_dim),
            grad_w_out.reshape(num_heads, head_dim, model_width),
        )

    return jax.shard_map(
        device_layer,
        mesh=mesh,
        in_specs=(row_spec, row_spec, rep_spec, rep_spec, rep_spec, rep_spec),
        out_specs=(row_spec, row_spec, part_spec, part_spec, part_spec, part_spec),
        check_vma=False,
    )
```

profile of v0, /device:TPU:21, one launch (start us, length us, event | category | flops | bytes accessed | tf_op | source)
XLA Modules:
  0.0 561.4 jit_solution(9339782933188814588)
XLA Ops:
  7.3 1.1 copy-done
  8.4 3.6 fusion.29
  12.0 1.3 fusion.30
  13.3 0.7 pad_maximum_fusion.1
  14.2 6.0 %fusion.22 = bf16[512,512]{0,1:T(8,128)(2,1)S(1)} fusion(bf16[512,4096]{1,0:T(8,128)(2,1)} %param.6, bf16[512,8,4,128]{3,2,1,0:T(4,128)(2,1)} %bitcast.167), kind=kOutput, calls=%fused_computation.33 | convolution fusion | flops 2147745792 | bytes 8912896 | tf_op jit(solution)/shard_map/dot_general | solution.py:38
  20.2 2.4 convolution_convert_fusion.1
  22.6 4.1 broadcast_compare_fusion
  26.7 31.3 %all-gather.3.cloned.1.call-done = bf16[2,8192,128]{2,1,0:T(8,128)(2,1)} async-done(((bf16[2,512,128]{2,1,0:T(8,128)(2,1)}), bf16[2,8192,128]{2,1,0:T(8,128)(2,1)}) %all-gather.3.cloned.1.call-update) | async-done | bytes 4194320 | tf_op jit(solution)/shard_map/all_gather | solution.py:43
  57.9 25.7 %fusion.2 = (f32[4,512]{1,0:T(4,128)S(1)}, f32[8192,512,4]{1,0,2:T(8,128)}) fusion(pred[512,8192]{0,1:T(8,128)(4,1)} %broadcast_compare_fusion, bf16[512,4,128]{0,2,1:T(8,128)(2,1)S(1)} %bitcast.171, bf16[2,8192,128]{2,1,0:T(8,128)(2,1)} %all-gather.3.cloned.1.call-done), kind=kOutput, calls=%fused_computation.6 | convolution fusion | flops 4345296896 | bytes 73932800 | tf_op jit(solution)/shard_map/tkgd,skd->kgts/dot_general | solution.py:45
  83.6 22.7 %exponential_reduce_fusion = f32[4,512]{1,0:T(4,128)S(1)} fusion(f32[8192,512,4]{1,0,2:T(8,128)} %get-tuple-element.17, f32[4,512]{1,0:T(4,128)S(1)} %is-finite_select_fusion, pred[512,8192]{0,1:T(8,128)(4,1)} %broadcast_compare_fusion), kind=kLoop, calls=%fused_computation.5 | loop fusion | flops 67106816 | bytes 71319552 | tf_op jit(solution)/shard_map/reduce_sum | solution.py:47
  106.4 34.7 %exponential_convert_fusion = bf16[1,4,512,8192]{2,3,1,0:T(8,128)(2,1)} fusion(f32[8192,512,4]{1,0,2:T(8,128)} %get-tuple-element.17, f32[4,512]{1,0:T(4,128)S(1)} %log_add_fusion, pred[512,8192]{0,1:T(8,128)(4,1)} %broadcast_compare_fusion), kind=kLoop, calls=%fused_computation.4 | loop fusion | flops 67108864 | bytes 104865792 | tf_op jit(solution)/shard_map/convert_element_type | solution.py:48
  141.1 17.6 %fusion.8 = f32[1,8192,1,128]{1,3,2,0:T(8,128)} fusion(bf16[512,4,128]{0,2,1:T(8,128)(2,1)S(1)} %bitcast.161, bf16[1,4,512,8192]{2,3,1,0:T(8,128)(2,1)} %exponential_convert_fusion), kind=kOutput, calls=%fused_computation.12 | convolution fusion | flops 4294967296 | bytes 38273024 | tf_op jit(solution)/shard_map/kgts,tkgd->skd/dot_general | solution.py:60
  158.7 15.7 %fusion.31 = (f32[4,512]{1,0:T(4,128)S(1)}, bf16[128,4,512]{2,0,1:T(8,128)(2,1)S(1)}) fusion(bf16[512,512]{0,1:T(8,128)(2,1)S(1)} %convolution_convert_fusion.1, bf16[1,4,512,8192]{2,3,1,0:T(8,128)(2,1)} %exponential_convert_fusion, bf16[2,8192,128]{2,1,0:T(8,128)(2,1)} %all-gather.3.cloned.1.call-done), kind=kOutput, calls=%fused_computation.42 | convolution fusion | flops 4296275968 | bytes 36708352 | tf_op jit(solution)/shard_map/kgts,skd->tkgd/dot_general | solution.py:49
  174.4 24.1 %fusion.3 = bf16[4,512,8192]{1,2,0:T(8,128)(2,1)} fusion(bf16[1,4,512,8192]{2,3,1,0:T(8,128)(2,1)} %exponential_convert_fusion, f32[4,512]{1,0:T(4,128)S(1)} %get-tuple-element.18, bf16[512,4,128]{0,2,1:T(8,128)(2,1)S(1)} %bitcast.162, bf16[2,8192,128]{2,1,0:T(8,128)(2,1)} %all-gather.3.cloned.1.call-done), kind=kOutput, calls=%fused_computation.7 | convolution fusion | flops 4362076160 | bytes 69738496 | tf_op jit(solution)/shard_map/tkgd,skd->kgts/dot_general | solution.py:55
  198.5 17.9 %fusion.12 = f32[1,8192,1,128]{1,3,2,0:T(8,128)} fusion(bf16[512,4,128]{0,2,1:T(8,128)(2,1)S(1)} %bitcast.172, bf16[4,512,8192]{1,2,0:T(8,128)(2,1)} %fusion.3), kind=kOutput, calls=%fused_computation.15 | convolution fusion | flops 4296015872 | bytes 38273024 | tf_op jit(solution)/shard_map/kgts,tkgd->skd/dot_general | solution.py:59
  216.4 7.8 %pad_maximum_fusion = f32[2,8192,1,128]{1,3,2,0:T(8,128)} fusion(f32[1,8192,1,128]{1,3,2,0:T(8,128)} %fusion.8, f32[1,8192,1,128]{1,3,2,0:T(8,128)} %fusion.12), kind=kLoop, calls=%fused_computation.16 | loop fusion | flops 2097152 | bytes 16777216 | tf_op jit(solution)/shard_map/stack | solution.py:61
  224.3 15.9 %fusion.25 = bf16[128,4,512]{2,0,1:T(8,128)(2,1)S(1)} fusion(bf16[4,512,8192]{1,2,0:T(8,128)(2,1)} %fusion.3, bf16[2,8192,128]{2,1,0:T(8,128)(2,1)} %all-gather.3.cloned.1.call-done), kind=kOutput, calls=%fused_computation.35 | convolution fusion | flops 4295491584 | bytes 36175872 | tf_op jit(solution)/shard_map/kgts,skd->tkgd/dot_general | solution.py:57
  240.2 5.7 %fusion.58 = f32[512,4096]{1,0:T(8,128)} fusion(bf16[512,512]{0,1:T(8,128)(2,1)S(1)} %bitcast.163, bf16[512,4096]{1,0:T(8,128)(2,1)S(1)} %copy-done.2), kind=kOutput, calls=%fused_computation.81 | convolution fusion | flops 2147483648 | bytes 13107200 | tf_op jit(solution)/shard_map/tm,te->me/dot_general | solution.py:70
  246.0 10.1 %copy.20 = f32[4096,4,128]{2,1,0:T(4,128)} copy(f32[4096,4,128]{0,2,1:T(8,128)} %bitcast.160) | data formatting | bytes 16777216 | tf_op jit(solution)/shard_map/reshape | solution.py:79
  256.1 7.9 %fusion.59 = f32[512,4096]{1,0:T(8,128)} fusion(bf16[512,512]{0,1:T(8,128)(2,1)S(1)} %bitcast.165, bf16[512,4096]{1,0:T(8,128)(2,1)} %param.7), kind=kOutput, calls=%fused_computation.82 | convolution fusion | flops 2147483648 | bytes 13107200 | tf_op jit(solution)/shard_map/te,tm->em/dot_general | solution.py:73
  264.0 22.9 %reduce-scatter.2.cloned.1.call-done = f32[2,512,1,128]{1,3,2,0:T(8,128)} async-done(((f32[2,8192,1,128]{1,3,2,0:T(8,128)}), f32[2,512,1,128]{1,3,2,0:T(8,128)}) %reduce-scatter.2.cloned.1.call-update) | async-done | bytes 524304 | tf_op jit(solution)/shard_map/reduce_scatter | solution.py:61
  286.9 4.5 convolution_bitcast_fusion.1
  291.4 2.0 convolution_bitcast_fusion.2
  293.5 6.7 %convolution_convert_fusion = bf16[512,4096]{1,0:T(8,128)(2,1)} fusion(bf16[512,512]{0,1:T(8,128)(2,1)S(1)} %bitcast.166, bf16[512,4096]{1,0:T(8,128)(2,1)} %bitcast.169), kind=kOutput, calls=%fused_computation.19 | convolution fusion | flops 2149580800 | bytes 8912896 | tf_op jit(solution)/shard_map/dot_general | solution.py:51
  300.2 2.4 fusion.13
  302.6 1.3 fusion.34
  303.9 3.4 add_convert_fusion
  307.3 222.8 %all-reduce.3.cloned.1.call-done = (f32[4096,4,128]{2,1,0:T(4,128)}, f32[4096,1,128]{0,2,1:T(8,128)}, f32[4096,1,128]{0,2,1:T(8,128)}, f32[4,128,4096]{2,1,0:T(8,128)}) async-done(((f32[4096,4,128]{2,1,0:T(4,128)}, f32[4096,1,128]{0,2,1:T(8,128)}, f32[4096,1,128]{0,2,1:T(8,128)}, f32[4,128,4096]{2,1,0:T(8,128)}), (f32[4096,4,128]{2,1,0:T(4,128)}, f32[4096,1,128]{0,2,1:T(8,128)}, f32[4096,1,128]{0,2,1:T(8,128)}, ...) | async-done | bytes 20971536 | tf_op jit(solution)/shard_map/psum | solution.py:75
  530.1 5.8 %copy.21 = f32[4096,1,128]{2,1,0:T(1,128)} copy(f32[4096,1,128]{0,2,1:T(8,128)} %get-tuple-element.13) | data formatting | bytes 4194304
  535.9 3.7 copy.22
  539.5 7.1 %copy.55 = f32[4096,4,128]{2,1,0:T(4,128)} copy(f32[4096,4,128]{2,1,0:T(4,128)} %get-tuple-element.22) | data formatting | bytes 16777216
  546.6 7.8 %copy.56 = f32[4,128,4096]{2,1,0:T(8,128)} copy(f32[4,128,4096]{2,1,0:T(8,128)} %get-tuple-element.25) | data formatting | bytes 16777216
  (31 shorter events, 0.4 us)
Async XLA Ops:
  7.2 1.2 copy-start
  7.2 4.8 copy-start.9
  7.2 50.7 %all-gather.3.cloned.1.call-start = ((), (), s32[]{:S(2)}) async-start(), calls=%async_computation.2 | async-start | bytes 4456448 | tf_op jit(solution)/shard_map/all_gather | solution.py:43
  8.4 3.6 copy-start.1
  14.1 272.8 %reduce-scatter.2.cloned.1.call-start = ((), (), s32[]{:S(2)}) async-start(), calls=%async_computation.1 | async-start | bytes 8912896 | tf_op jit(solution)/shard_map/reduce_scatter | solution.py:61
  14.2 6.0 %copy-start.4 = (bf16[512,4096]{1,0:T(8,128)(2,1)S(1)}, bf16[512,4096]{1,0:T(8,128)(2,1)}, u32[]{:S(2)}) copy-start(bf16[512,4096]{1,0:T(8,128)(2,1)} %param.7) | copy-start | bytes 12582916
  14.2 6.0 %copy-start.6 = (bf16[4,128,4096]{2,1,0:T(8,128)(2,1)S(1)}, bf16[4,128,4096]{2,1,0:T(8,128)(2,1)}, u32[]{:S(2)}) copy-start(bf16[4,128,4096]{2,1,0:T(8,128)(2,1)} %param.11) | copy-start | bytes 12582916
  224.3 305.8 %all-reduce.3.cloned.1.call-start = ((), (), s32[]{:S(2)}) async-start(), calls=%async_computation.3 | async-start | bytes 41943040 | tf_op jit(solution)/shard_map/psum | solution.py:75
  224.3 15.9 %copy-start.2 = (bf16[512,4096]{1,0:T(8,128)(2,1)S(1)}, bf16[512,4096]{1,0:T(8,128)(2,1)}, u32[]{:S(2)}) copy-start(bf16[512,4096]{1,0:T(8,128)(2,1)} %param.6) | copy-start | bytes 12582916
  286.9 4.5 copy-start.3
  286.9 4.5 copy-start.7
  293.5 6.7 %copy-start.5 = (bf16[4096,4,128]{2,1,0:T(4,128)(2,1)S(1)}, bf16[4096,4,128]{2,1,0:T(4,128)(2,1)}, u32[]{:S(2)}) copy-start(bf16[4096,4,128]{2,1,0:T(4,128)(2,1)} %param.8) | copy-start | bytes 12582916
  302.6 1.3 copy-start.10
  530.1 5.8 %copy-start.8 = (f32[4096,1,128]{0,2,1:T(8,128)S(1)}, f32[4096,1,128]{0,2,1:T(8,128)}, u32[]{:S(2)}) copy-start(f32[4096,1,128]{0,2,1:T(8,128)} %get-tuple-element.14) | copy-start | bytes 6291460
Sparse Core Ops, SparseCore 0:
  14.2 43.6 all-gather.2
  224.4 62.4 reduce-scatter.1
  293.6 236.4 all-reduce.2
where the time goes:
time: 567 us; the launch traced here: 561 us
  waiting for transfers between devices  277 us (49%)
  matrix products  164 us (29%)
  other arithmetic  70.1 us (12%)
  local copies, waits for them, and re-layouts  35.7 us (6%)
  between operations  14.4 us (3%)
    psum x1, waiting for transfers between devices, device_layer(): lax.psum(weight_parts, 'cp')  223 us
    convert_element_type x1, other arithmetic, device_layer(): att_probs = jnp.exp(masked - log_norm[..., None]).astype(jnp.bfloat16)  34.7 us
    all_gather x1, waiting for transfers between devices, device_layer(): kv_all = lax.all_gather(kv_local, 'cp', axis=1, tiled=True)  31.3 us
    dot_general x1, matrix products, device_layer(): jnp.einsum('tkgd,skd->kgts', query_heads, key_rows, preferred_element_typ...  25.7 us
    unnamed x26, local copies, waits for them, and re-layouts  25.5 us
    dot_general x1, matrix products, device_layer(): jnp.einsum('tkgd,skd->kgts', dout_heads, value_rows, preferred_element_ty...  24.1 us
    reduce_scatter x1, waiting for transfers between devices, device_layer(): lax.psum_scatter(jnp.stack([key_part, value_part]), 'cp', scatter_dimensi...  22.9 us
    reduce_sum x1, other arithmetic, device_layer(): log_norm = jax.nn.logsumexp(masked, axis=-1)  22.7 us
  transfers between devices with their start and end apart: 3, of which 3 were waited for; matrix products, arithmetic and copies ran while one was open for 12% of the time, Pallas kernels for 0%

commit v1 on v0

v1 whole, which is shorter than its diff:
```python
import functools
import math

import jax
import jax.numpy as jnp
from jax import lax
from jax.experimental import pallas as pl
from jax.experimental.pallas import tpu as pltpu
from jax.sharding import PartitionSpec as P

F32 = jnp.float32
BF16 = jnp.bfloat16
MESH = pl.DeviceIdType.MESH
HBM = pl.BlockSpec(memory_space=pl.ANY)


def dot(a, b):
    return jnp.dot(a, b, preferred_element_type=F32)


def dot_nt(a, b):
    return lax.dot_general(a, b, (((1,), (1,)), ((), ())), preferred_element_type=F32)


def layer_kernel(
    n, heads, x_hbm, dy_hbm, wq_hbm, wk_hbm, wv_hbm, wo_hbm,
    y_hbm, dx_hbm, gq_hbm, gk_hbm, gv_hbm, go_hbm,
    x, dy, wqkv, wo, kv, q_rows, q_cols, do_rows, do_cols, o_rows, o_cols,
    acc, m_state, l_state, delta, dqkv, p_cols, ds_cols, slot_o, part_o, arena, part_w, x_cols, stage,
    in_sem, kv_send, kv_recv, ro_send, ro_recv, go_send, go_recv, rkv_send, rkv_recv,
    rw_send, rw_recv, gw_send, gw_recv, out_o_sem, out_w_sem, stage_sem, ready_sem,
):
    tok, width = x.shape
    half = tok // 2
    embed = wo.shape[0]
    hd = embed // heads
    kvw = wqkv.shape[1] - embed
    mc = width // n
    me_half = mc // 2
    cols = heads * half
    scale = hd ** -0.5
    scale2 = scale * math.log2(math.e)
    steps_right = n // 2
    steps_left = n - 1 - n // 2
    me = lax.axis_index("cp")
    right = lax.rem(me + 1, n)
    left = lax.rem(me + n - 1, n)
    target = (right, left)

    def wrap(i):
        return lax.rem(i + 2 * n, n)

    def rcopy(src, dst, send, recv, direction):
        return pltpu.make_async_remote_copy(
            src_ref=src, dst_ref=dst, send_sem=send, recv_sem=recv,
            device_id={"cp": target[direction]}, device_id_type=MESH,
        )

    def rs_chunk(direction, t):
        return wrap(me - 1 - t) if direction == 0 else wrap(me + 1 + t)

    def ag_chunk(direction, t):
        return wrap(me - t) if direction == 0 else wrap(me + t)

    loads = [
        pltpu.make_async_copy(x_hbm, x, in_sem.at[0]),
        pltpu.make_async_copy(wk_hbm, wqkv.at[:, pl.ds(embed, kvw // 2)], in_sem.at[1]),
        pltpu.make_async_copy(wv_hbm, wqkv.at[:, pl.ds(embed + kvw // 2, kvw // 2)], in_sem.at[2]),
        pltpu.make_async_copy(wq_hbm, wqkv.at[:, pl.ds(0, embed)], in_sem.at[3]),
        pltpu.make_async_copy(dy_hbm, dy, in_sem.at[4]),
        pltpu.make_async_copy(wo_hbm, wo, in_sem.at[5]),
    ]
    for load in loads:
        load.start()

    barrier = pltpu.get_barrier_semaphore()
    for device in target:
        pl.semaphore_signal(barrier, inc=1, device_id={"cp": device}, device_id_type=MESH)

    for load in loads[:3]:
        load.wait()

    kv[me] = dot(x[...], wqkv[:, embed:]).astype(BF16)
    pl.semaphore_wait(barrier, 2)

    def kv_copy(direction, t):
        c = ag_chunk(direction, t)
        return rcopy(kv.at[c], kv.at[c], kv_send.at[direction, t], kv_recv.at[direction, t], direction)

    def kv_tick(t):
        for direction, steps in ((0, steps_right), (1, steps_left)):
            @pl.when(t < steps)
            def _(direction=direction, steps=steps):
                kv_copy(direction, t).wait_recv()

                @pl.when(t + 1 < steps)
                def _():
                    kv_copy(direction, t + 1).start()

    for direction in (0, 1):
        kv_copy(direction, 0).start()

    def spread(block, rows_ref, cols_ref, h):
        for b in range(2):
            piece = block[b * half:(b + 1) * half]
            rows_ref[b, h * half:(h + 1) * half, :] = piece
            cols_ref[b, :, h * half:(h + 1) * half] = piece.T

    per = 256 // hd

    def project_q(g):
        block = dot(x[...], wqkv[:, g * 256:(g + 1) * 256]).astype(BF16)
        for i in range(per):
            spread(block[:, i * hd:(i + 1) * hd], q_rows, q_cols, g * per + i)

    def project_do(g):
        block = dot_nt(dy[...], wo[g * 256:(g + 1) * 256, :]).astype(BF16)
        for i in range(per):
            spread(block[:, i * hd:(i + 1) * hd], do_rows, do_cols, g * per + i)

    loads[3].wait()
    for g in range(embed // 256):
        project_q(g)
        if g == 0:
            kv_tick(0)
    loads[4].wait()
    loads[5].wait()
    for g in range(embed // 256):
        project_do(g)
        if g == 0:
            kv_tick(1)
    early = 2

    m_state[...] = jnp.full(m_state.shape, -jnp.inf, F32)
    l_state[...] = jnp.zeros(l_state.shape, F32)
    acc[...] = jnp.zeros(acc.shape, F32)

    def diagonal():
        key_id = lax.broadcasted_iota(jnp.int32, (half, half), 0)
        query_id = lax.broadcasted_iota(jnp.int32, (half, half), 1)
        return key_id <= query_id

    def forward_unit(s, qb, kb, masked):
        keys = kv[s, pl.ds(kb * half, half), :hd]
        values_t = kv[s, pl.ds(kb * half, half), hd:].T
        for h in range(heads):
            lanes = slice(h * half, (h + 1) * half)
            sc = dot(keys, q_cols[qb, :, lanes])
            if masked:
                sc = jnp.where(diagonal(), sc, -jnp.inf)
            old = m_state[qb, :, lanes]
            new = jnp.maximum(old, jnp.max(sc, axis=0, keepdims=True) * scale2)
            fade = jnp.exp2(old - new)
            p = jnp.exp2(sc * scale2 - new)
            l_state[qb, :, lanes] = l_state[qb, :, lanes] * fade + jnp.sum(p, axis=0, keepdims=True)
            m_state[qb, :, lanes] = new
            acc[qb, :, lanes] = acc[qb, :, lanes] * fade + dot(values_t, p.astype(BF16))

    forward_unit(me, 1, 0, False)
    forward_unit(me, 0, 0, True)
    forward_unit(me, 1, 1, True)

    def unit_blocks(s, u):
        same = jnp.where(s < me, 0, 1)
        return jnp.where(u == 0, 1, same), jnp.where(u == 0, 0, same)

    def forward_step(j, carry):
        k = j // 2

        @pl.when(lax.rem(j, 2) == 0)
        def _():
            kv_tick(k + early)

        s = jnp.where(lax.rem(j, 2) == 0, wrap(me - 1 - k), wrap(me + 1 + k))

        def unit(u, c):
            qb, kb = unit_blocks(s, u)
            forward_unit(s, qb, kb, False)
            return c

        return lax.fori_loop(0, 2, unit, carry)

    lax.fori_loop(0, n - 1, forward_step, 0)

    for direction, steps in ((0, steps_right), (1, steps_left)):
        def drain(t, c, direction=direction):
            kv_copy(direction, t).wait_send()
            return c
        lax.fori_loop(0, steps, drain, 0)

    for b in range(2):
        for h in range(heads):
            lanes = slice(h * half, (h + 1) * half)
            total = l_state[b, :, lanes]
            out = (acc[b, :, lanes] / total).astype(BF16)
            o_cols[h * hd:(h + 1) * hd, b * half:(b + 1) * half] = out
            o_rows[b * half:(b + 1) * half, h * hd:(h + 1) * hd] = out.T
            delta[b, :, lanes] = jnp.sum(
                out.astype(F32) * do_cols[b, :, lanes].astype(F32), axis=0, keepdims=True
            )
            m_state[b, :, lanes] = m_state[b, :, lanes] + jnp.log(total) * math.log2(math.e)

    eh = embed // 2

    def wo_part(t):
        for direction in (0, 1):
            c = rs_chunk(direction, t)
            at = pl.ds(pl.multiple_of(c * mc, mc), mc)
            part_o[direction] = dot(o_cols[direction * eh:(direction + 1) * eh, :], dy[:, at])

    def ro_copy(direction, t):
        c = rs_chunk(direction, t)
        return rcopy(slot_o.at[direction, c], slot_o.at[direction, c],
                     ro_send.at[direction, t], ro_recv.at[direction, t], direction)

    def wait_sends(copy, t):
        for direction in (0, 1):
            copy(direction, t).wait_send()

    def ro_tick(t):
        for direction in (0, 1):
            c = rs_chunk(direction, t)
            ro_copy(direction, t - 1).wait_recv()
            slot_o[direction, c] = slot_o[direction, c] + part_o[direction]

    wo_part(0)
    for direction in (0, 1):
        slot_o[direction, rs_chunk(direction, 0)] = part_o[direction]
        ro_copy(direction, 0).start()
    wo_part(1)

    part_kv0 = 0
    slot_kv0 = 2 * n * tok

    def kv_rows(base, direction, c):
        return pl.multiple_of(base + (direction * n + c) * tok, tok)

    acc[...] = jnp.zeros(acc.shape, F32)

    def backward_unit(s, qb, kb, masked, add):
        keys = kv[s, pl.ds(kb * half, half), :hd]
        values = kv[s, pl.ds(kb * half, half), hd:]
        keys_t = keys.T
        for h in range(heads):
            lanes = slice(h * half, (h + 1) * half)
            sc = dot(keys, q_cols[qb, :, lanes])
            p = jnp.exp2(sc * scale2 - m_state[qb, :, lanes])
            if masked:
                p = jnp.where(diagonal(), p, 0.0)
            p = p.astype(BF16)
            p_cols[:, lanes] = p
            dp = dot(values, do_cols[qb, :, lanes])
            ds = (p.astype(F32) * (dp - delta[qb, :, lanes])).astype(BF16)
            ds_cols[:, lanes] = ds
            acc[qb, :, lanes] = acc[qb, :, lanes] + dot(keys_t, ds)
        for direction, lhs, rhs in ((0, ds_cols, q_rows), (1, p_cols, do_rows)):
            rows = pl.ds(pl.multiple_of(kv_rows(part_kv0, direction, s) + kb * half, half), half)
            g = dot(lhs[...], rhs[qb])
            arena[rows, :] = arena[rows, :] + g if add else g

    def zero_block(s, kb):
        for direction in (0, 1):
            rows = pl.ds(pl.multiple_of(kv_rows(part_kv0, direction, s) + kb * half, half), half)
            arena[rows, :] = jnp.zeros((half, hd), F32)

    backward_unit(me, 1, 0, False, False)
    backward_unit(me, 0, 0, True, True)
    backward_unit(me, 1, 1, True, False)

    def backward_step(j, carry):
        s = wrap(me + j)

        @pl.when(jnp.logical_and(j >= 2, j < n - 1))
        def _():
            wait_sends(ro_copy, j - 2)

        @pl.when(j < n - 1)
        def _():
            ro_tick(j)
            for direction in (0, 1):
                ro_copy(direction, j).start()
            wo_part(j + 1)

        zero_block(s, 0)
        zero_block(s, 1)

        def unit(u, c):
            qb, kb = unit_blocks(s, u)
            backward_unit(s, qb, kb, False, True)
            return c

        return lax.fori_loop(0, 2, unit, carry)

    lax.fori_loop(1, n, backward_step, 0)

    for b in range(2):
        for h in range(heads):
            g = (acc[b, :, h * half:(h + 1) * half] * scale).astype(BF16)
            dqkv[b * half:(b + 1) * half, h * hd:(h + 1) * hd] = g.T

    def rkv_copy(direction, t):
        rows = pl.ds(kv_rows(slot_kv0, direction, rs_chunk(direction, t)), tok)
        return rcopy(arena.at[rows], arena.at[rows], rkv_send.at[direction, t], rkv_recv.at[direction, t], direction)

    def rkv_add(direction, c):
        slot = pl.ds(kv_rows(slot_kv0, direction, c), tok)
        part = pl.ds(kv_rows(part_kv0, direction, c), tok)
        return arena[slot, :] + arena[part, :]

    def go_copy(direction, t):
        c = ag_chunk(direction, t)
        return rcopy(slot_o.at[direction, c], slot_o.at[direction, c],
                     go_send.at[direction, t], go_recv.at[direction, t], direction)

    def go_out(direction, t):
        c = ag_chunk(direction, t)
        return pltpu.make_async_copy(
            slot_o.at[direction, c],
            go_hbm.at[pl.ds(direction * eh, eh), pl.ds(pl.multiple_of(c * mc, mc), mc)],
            out_o_sem.at[direction, t],
        )

    def stage_copy(dst, i):
        return pltpu.make_async_copy(
            stage.at[lax.rem(i, 2)], dst.at[:, pl.ds(pl.multiple_of(i * mc, mc), mc)], stage_sem.at[lax.rem(i, 2)]
        )

    def y_piece(i):
        stage[lax.rem(i, 2)] = dot(o_rows[...], wo[:, pl.ds(pl.multiple_of(i * mc, mc), mc)]).astype(BF16)
        stage_copy(y_hbm, i).start()

    for direction in (0, 1):
        c = rs_chunk(direction, 0)
        arena[pl.ds(kv_rows(slot_kv0, direction, c), tok), :] = arena[pl.ds(kv_rows(part_kv0, direction, c), tok), :]
        rkv_copy(direction, 0).start()
    ro_tick(n - 1)
    for direction in (0, 1):
        go_copy(direction, 0).start()
        go_out(direction, 0).start()
    y_piece(0)
    y_piece(1)

    def second_step(t, carry):
        for direction in (0, 1):
            c = rs_chunk(direction, t)
            rkv_copy(direction, t - 1).wait_recv()
            arena[pl.ds(kv_rows(slot_kv0, direction, c), tok), :] = rkv_add(direction, c)
            rkv_copy(direction, t).start()

        @pl.when(t <= 2)
        def _():
            wait_sends(ro_copy, n - 4 + t)

        for direction in (0, 1):
            go_copy(direction, t - 1).wait_recv()
            go_copy(direction, t).start()
            go_out(direction, t).start()
        stage_copy(y_hbm, t - 1).wait()
        y_piece(t + 1)
        return carry

    lax.fori_loop(1, n - 1, second_step, 0)

    for direction in (0, 1):
        rkv_copy(direction, n - 2).wait_recv()
        g = rkv_add(direction, me)
        if direction == 0:
            g = g * scale
        dqkv[:, embed + direction * hd:embed + (direction + 1) * hd] = g.astype(BF16)

    def drain_kv(t, c):
        for direction in (0, 1):
            rkv_copy(direction, t).wait_send()
        return c

    lax.fori_loop(0, n - 1, drain_kv, 0)
    for device in target:
        pl.semaphore_signal(ready_sem, inc=1, device_id={"cp": device}, device_id_type=MESH)

    wrow = me_half * (heads + 2)

    def w_rows(direction, c):
        return pl.multiple_of((direction * n + c) * wrow, wrow)

    def w_part(t):
        for direction in (0, 1):
            c = rs_chunk(direction, t)
            at = pl.ds(pl.multiple_of(c * mc + direction * me_half, me_half), me_half)
            x_cols[...] = x[:, at].T
            for g in range((embed + kvw) // 256):
                block = dot(x_cols[...], dqkv[:, g * 256:(g + 1) * 256])
                for i in range(per):
                    h = g * per + i
                    piece = block[:, i * hd:(i + 1) * hd]
                    if h < heads:
                        part_w[direction, pl.ds(h, me_half, stride=heads), :] = piece
                    else:
                        part_w[direction, pl.ds(h * me_half, me_half), :] = piece

    def rw_copy(direction, t):
        rows = pl.ds(w_rows(direction, rs_chunk(direction, t)), wrow)
        return rcopy(arena.at[rows], arena.at[rows], rw_send.at[direction, t], rw_recv.at[direction, t], direction)

    def rw_tick(t):
        for direction in (0, 1):
            rows = pl.ds(w_rows(direction, rs_chunk(direction, t)), wrow)
            rw_copy(direction, t - 1).wait_recv()
            arena[rows, :] = arena[rows, :] + part_w[direction]

    def gw_copy(direction, t):
        rows = pl.ds(w_rows(direction, ag_chunk(direction, t)), wrow)
        return rcopy(arena.at[rows], arena.at[rows], gw_send.at[direction, t], gw_recv.at[direction, t], direction)

    def gw_out(direction, t):
        c = ag_chunk(direction, t)
        row = w_rows(direction, c)
        first = c * mc + direction * me_half
        return [
            pltpu.make_async_copy(
                arena.at[pl.ds(row + skip * me_half, rows * me_half)],
                dst.at[pl.ds(pl.multiple_of(first * rows, me_half), rows * me_half)],
                out_w_sem.at[direction, t, k],
            )
            for k, (dst, skip, rows) in enumerate(((gq_hbm, 0, heads), (gk_hbm, heads, 1), (gv_hbm, heads + 1, 1)))
        ]

    w_part(0)
    pl.semaphore_wait(ready_sem, 2)
    for direction in (0, 1):
        arena[pl.ds(w_rows(direction, rs_chunk(direction, 0)), wrow), :] = part_w[direction]
        rw_copy(direction, 0).start()
    w_part(1)

    for direction in (0, 1):
        go_copy(direction, n - 2).wait_recv()
        go_out(direction, n - 1).start()
    stage_copy(y_hbm, n - 2).wait()
    stage_copy(y_hbm, n - 1).wait()

    def third_step(t, carry):
        @pl.when(t >= 2)
        def _():
            wait_sends(rw_copy, t - 2)

        rw_tick(t)
        for direction in (0, 1):
            rw_copy(direction, t).start()
        w_part(t + 1)
        return carry

    lax.fori_loop(1, n - 1, third_step, 0)

    def dx_piece(i):
        at = pl.ds(pl.multiple_of(i * mc, mc), mc)
        stage[lax.rem(i, 2)] = dot_nt(dqkv[...], wqkv[at, :]).astype(BF16)
        stage_copy(dx_hbm, i).start()

    rw_tick(n - 1)
    for direction in (0, 1):
        gw_copy(direction, 0).start()
        for copy in gw_out(direction, 0):
            copy.start()
    dx_piece(0)
    dx_piece(1)

    def fourth_step(t, carry):
        @pl.when(t <= 2)
        def _():
            wait_sends(rw_copy, n - 4 + t)

        for direction in (0, 1):
            gw_copy(direction, t - 1).wait_recv()
            gw_copy(direction, t).start()
            for copy in gw_out(direction, t):
                copy.start()
        stage_copy(dx_hbm, t - 1).wait()
        dx_piece(t + 1)
        return carry

    lax.fori_loop(1, n - 1, fourth_step, 0)

    stage_copy(dx_hbm, n - 2).wait()
    stage_copy(dx_hbm, n - 1).wait()

    def drain_all(t, c):
        for direction in (0, 1):
            go_copy(direction, t).wait_send()
            gw_copy(direction, t).wait_send()
            go_out(direction, t).wait()
        return c

    lax.fori_loop(0, n - 1, drain_all, 0)
    for direction in (0, 1):
        go_out(direction, n - 1).wait()
        gw_copy(direction, n - 2).wait_recv()
        for copy in gw_out(direction, n - 1):
            copy.start()

    def drain_out(t, c):
        for direction in (0, 1):
            for copy in gw_out(direction, t):
                copy.wait()
        return c

    lax.fori_loop(0, n, drain_out, 0)


def solution(mesh):
    n = mesh.shape["cp"]
    row_spec = P(("dp", "cp"), None)
    rep_spec = P(None, None, None)
    part_spec = P("dp", None, None)

    def device_layer(hidden, grad_out, w_query, w_key, w_value, w_out):
        tok, width = hidden.shape
        heads, hd = w_query.shape[1], w_query.shape[2]
        embed = heads * hd
        kvw = 2 * hd
        half = tok // 2
        cols = heads * half
        mc = width // n
        wrow = mc // 2 * (heads + 2)
        dma = lambda *shape: pltpu.SemaphoreType.DMA(shape)
        ring = dma(2, n - 1)
        outs = pl.pallas_call(
            functools.partial(layer_kernel, n, heads),
            name="attention_layer",
            out_shape=[
                jax.ShapeDtypeStruct((tok, width), BF16),
                jax.ShapeDtypeStruct((tok, width), BF16),
                jax.ShapeDtypeStruct((width * heads, hd), F32),
                jax.ShapeDtypeStruct((width, hd), F32),
                jax.ShapeDtypeStruct((width, hd), F32),
                jax.ShapeDtypeStruct((embed, width), F32),
            ],
            in_specs=[HBM] * 6,
            out_specs=[HBM] * 6,
            scratch_shapes=[
                pltpu.VMEM((tok, width), BF16),
                pltpu.VMEM((tok, width), BF16),
                pltpu.VMEM((width, embed + kvw), BF16),
                pltpu.VMEM((embed, width), BF16),
                pltpu.VMEM((n, tok, kvw), BF16),
                pltpu.VMEM((2, cols, hd), BF16),
                pltpu.VMEM((2, hd, cols), BF16),
                pltpu.VMEM((2, cols, hd), BF16),
                pltpu.VMEM((2, hd, cols), BF16),
                pltpu.VMEM((tok, embed), BF16),
                pltpu.VMEM((embed, tok), BF16),
                pltpu.VMEM((2, hd, cols), F32),
                pltpu.VMEM((2, 1, cols), F32),
                pltpu.VMEM((2, 1, cols), F32),
                pltpu.VMEM((2, 1, cols), F32),
                pltpu.VMEM((tok, embed + kvw), BF16),
                pltpu.VMEM((half, cols), BF16),
                pltpu.VMEM((half, cols), BF16),
                pltpu.VMEM((2, n, embed // 2, mc), F32),
                pltpu.VMEM((2, embed // 2, mc), F32),
                pltpu.VMEM((max(4 * n * tok, 2 * n * wrow), hd), F32),
                pltpu.VMEM((2, wrow, hd), F32),
                pltpu.VMEM((mc // 2, tok), BF16),
                pltpu.VMEM((2, tok, mc), BF16),
                dma(6),
                dma(2, n // 2), dma(2, n // 2),
                ring, ring, ring, ring, ring, ring, ring, ring, ring, ring,
                dma(2, n), dma(2, n, 3), dma(2),
                pltpu.SemaphoreType.REGULAR,
            ],
            compiler_params=pltpu.CompilerParams(
                collective_id=0, has_side_effects=True, vmem_limit_bytes=67_000_000
            ),
        )(
            hidden, grad_out, w_query.reshape(width, embed), w_key.reshape(width, hd), w_value.reshape(width, hd),
            w_out.reshape(embed, width),
        )
        output, grad_hidden, gq, gk, gv, go = outs
        return (
            output,
            grad_hidden,
            gq.reshape(width, heads, hd),
            gk.reshape(width, 1, hd),
            gv.reshape(width, 1, hd),
            go.reshape(heads, hd, width),
        )

    return jax.shard_map(
        device_layer,
        mesh=mesh,
        in_specs=(row_spec, row_spec, rep_spec, rep_spec, rep_spec, rep_spec),
        out_specs=(row_spec, row_spec, part_spec, part_spec, part_spec, part_spec),
        check_vma=False,
    )
```

time: 567 us -> 448 us (0.79)
  Pallas kernels: 0 us -> 420 us
  waiting for transfers between devices: 277 us -> 0 us
  matrix products: 164 us -> 0 us
  other arithmetic: 70.1 us -> 0.01 us
  between operations: 14.4 us -> 0.66 us
  local copies, waits for them, and re-layouts: 35.7 us -> 26.8 us
    pallas_call x0 -> x1, Pallas kernels: none -> 420 us  [device_layer(): pl.pallas_call(functools.partial(layer_kernel, n, heads), name='attention...]
    psum x1 -> x0, waiting for transfers between devices: 223 us -> none  [device_layer(): lax.psum(weight_parts, 'cp')]
    dot_general x18 -> x0, matrix products: 164 us -> none  [the longest x1 25.7 us: device_layer(): jnp.einsum('tkgd,skd->kgts', query_heads, key_rows, preferred_element_typ...]
    convert_element_type x1 -> x0, other arithmetic: 34.7 us -> none  [device_layer(): att_probs = jnp.exp(masked - log_norm[..., None]).astype(jnp.bfloat16)]
    all_gather x1 -> x0, waiting for transfers between devices: 31.3 us -> none  [device_layer(): kv_all = lax.all_gather(kv_local, 'cp', axis=1, tiled=True)]
    reduce_scatter x1 -> x0, waiting for transfers between devices: 22.9 us -> none  [device_layer(): lax.psum_scatter(jnp.stack([key_part, value_part]), 'cp', scatter_dimensi...]
    reduce_sum x1 -> x0, other arithmetic: 22.7 us -> none  [device_layer(): log_norm = jax.nn.logsumexp(masked, axis=-1)]
    reshape x1 -> x0, local copies, waits for them, and re-layouts: 10.1 us -> none  [device_layer(): grad_w_query.reshape(model_width, num_heads, head_dim)]
  transfers between devices with their start and end apart: 3 -> 0, of which waited for: 3 -> 0; matrix products, arithmetic and copies ran while one was open for 12% -> 0% of each run, Pallas kernels for 0% -> 0%
where the time goes in v1:
time: 448 us
  Pallas kernels  420 us (94%)
  local copies, waits for them, and re-layouts  26.8 us (6%)
    pallas_call x1, Pallas kernels, device_layer(): pl.pallas_call(functools.partial(layer_kernel, n, heads), name='attention...  420 us
    unnamed x17, local copies, waits for them, and re-layouts  26.8 us

profile of v1, /device:TPU:21, one launch (start us, length us, event | category | flops | bytes accessed | tf_op | source)
XLA Modules:
  0.0 447.8 jit_solution(7144059962501486220)
XLA Ops:
  0.6 4.9 %copy.16 = bf16[512,8,4,128]{3,1,2,0:T(8,128)(2,1)} copy(bf16[512,8,4,128]{3,2,1,0:T(4,128)(2,1)} %bitcast.20) | data formatting | bytes 8388608
  5.6 420.4 %attention_layer.1 = (bf16[512,4096]{1,0:T(8,128)(2,1)}, bf16[512,4096]{1,0:T(8,128)(2,1)}, f32[16384,128]{1,0:T(8,128)}, f32[4096,128]{1,0:T(8,128)}, f32[4096,128]{1,0:T(8,128)}, /*index=5*/f32[512,4096]{1,0:T(8,128)}) custom-call(bf16[512,4096]{1,0:T(8,128)(2,1)} %x_hbm.1, bf16[512,4096]{1,0:T(8,128)(2,1)} %dy_hbm.1, bf16[4096,512]{1,0:T(8,128)(2,1)} %bitcast.15, ...), custom_call_target="tpu_custom_call" | custom-call | tf_op jit(solution)/shard_map/attention_layer/pallas_call | solution.py:525
  426.0 0.0 copy-start
  426.0 5.0 %copy.23 = bf16[512,4096]{1,0:T(8,128)(2,1)} copy(bf16[512,4096]{1,0:T(8,128)(2,1)} %get-tuple-element.30) | data formatting | bytes 8388608
  430.9 0.0 slice-start
  431.0 4.9 %copy.24 = bf16[512,4096]{1,0:T(8,128)(2,1)} copy(bf16[512,4096]{1,0:T(8,128)(2,1)} %get-tuple-element.31) | data formatting | bytes 8388608
  435.8 0.0 copy-done
  435.8 0.0 copy-start.2
  435.8 0.0 slice-start.1
  435.8 4.3 copy.25
  440.1 0.0 copy-done.2
  440.1 0.0 copy-start.1
  440.1 1.3 copy.26
  441.4 1.7 copy-done.1
  443.1 1.3 copy.27
  444.4 0.0 slice-done
  444.4 0.0 slice-done.1
  444.4 3.4 copy.28
  (1 shorter events, 0.0 us)
Async XLA Ops:
  426.0 9.9 %copy-start = (f32[16384,128]{1,0:T(8,128)S(1)}, f32[16384,128]{1,0:T(8,128)}, u32[]{:S(2)}) copy-start(f32[16384,128]{1,0:T(8,128)} %get-tuple-element.14) | copy-start | bytes 25165828
  430.9 13.5 %slice-start = ((s8[8388608]{0:T(1024)(128)(4,1)}), s8[4194304]{0:T(1024)(128)(4,1)S(1)}, s32[]{:S(2)}) async-start(s8[8388608]{0:T(1024)(128)(4,1)} %bitcast.16), calls=%async_computation | async-start | bytes 8388608
  435.8 4.3 copy-start.2
  435.8 8.6 %slice-start.1 = ((s8[8388608]{0:T(1024)(128)(4,1)}), s8[4194304]{0:T(1024)(128)(4,1)S(1)}, s32[]{:S(2)}) async-start(s8[8388608]{0:T(1024)(128)(4,1)} %bitcast.16), calls=%async_computation.1 | async-start | bytes 8388608
  440.1 3.0 copy-start.1

commit v2 on v1

--- a/solution.py
+++ b/solution.py
@@ -40,12 +40,12 @@
     cols = heads * half
     scale = hd ** -0.5
     scale2 = scale * math.log2(math.e)
-    steps_right = n // 2
-    steps_left = n - 1 - n // 2
     me = lax.axis_index("cp")
     right = lax.rem(me + 1, n)
     left = lax.rem(me + n - 1, n)
-    target = (right, left)
+    second = lax.rem(me, 2)
+    first = 1 - second
+    order = (first, second)
 
     def wrap(i):
         return lax.rem(i + 2 * n, n)
@@ -53,14 +53,14 @@
     def rcopy(src, dst, send, recv, direction):
         return pltpu.make_async_remote_copy(
             src_ref=src, dst_ref=dst, send_sem=send, recv_sem=recv,
-            device_id={"cp": target[direction]}, device_id_type=MESH,
+            device_id={"cp": right + direction * (left - right)}, device_id_type=MESH,
         )
 
     def rs_chunk(direction, t):
-        return wrap(me - 1 - t) if direction == 0 else wrap(me + 1 + t)
+        return wrap(me + (2 * direction - 1) * (t + 1))
 
     def ag_chunk(direction, t):
-        return wrap(me - t) if direction == 0 else wrap(me + t)
+        return wrap(me + (2 * direction - 1) * t)
 
     loads = [
         pltpu.make_async_copy(x_hbm, x, in_sem.at[0]),
@@ -74,7 +74,7 @@
         load.start()
 
     barrier = pltpu.get_barrier_semaphore()
-    for device in target:
+    for device in (left, right):
         pl.semaphore_signal(barrier, inc=1, device_id={"cp": device}, device_id_type=MESH)
 
     for load in loads[:3]:
@@ -87,17 +87,19 @@
         c = ag_chunk(direction, t)
         return rcopy(kv.at[c], kv.at[c], kv_send.at[direction, t], kv_recv.at[direction, t], direction)
 
-    def kv_tick(t):
-        for direction, steps in ((0, steps_right), (1, steps_left)):
-            @pl.when(t < steps)
-            def _(direction=direction, steps=steps):
-                kv_copy(direction, t).wait_recv()
-
-                @pl.when(t + 1 < steps)
-                def _():
-                    kv_copy(direction, t + 1).start()
-
-    for direction in (0, 1):
+    def kv_steps(direction):
+        return n // 2 + direction * (n - 1 - 2 * (n // 2))
+
+    def kv_tick(direction, t):
+        @pl.when(t < kv_steps(direction))
+        def _():
+            kv_copy(direction, t).wait_recv()
+
+            @pl.when(t + 1 < kv_steps(direction))
+            def _():
+                kv_copy(direction, t + 1).start()
+
+    for direction in order:
         kv_copy(direction, 0).start()
 
     def spread(block, rows_ref, cols_ref, h):
@@ -121,15 +123,13 @@
     loads[3].wait()
     for g in range(embed // 256):
         project_q(g)
-        if g == 0:
-            kv_tick(0)
+        kv_tick(order[g % 2], g // 2)
     loads[4].wait()
     loads[5].wait()
     for g in range(embed // 256):
         project_do(g)
-        if g == 0:
-            kv_tick(1)
-    early = 2
+        kv_tick(order[g % 2], embed // 512 + g // 2)
+    early = embed // 256
 
     m_state[...] = jnp.full(m_state.shape, -jnp.inf, F32)
     l_state[...] = jnp.zeros(l_state.shape, F32)
@@ -165,13 +165,9 @@
         return jnp.where(u == 0, 1, same), jnp.where(u == 0, 0, same)
 
     def forward_step(j, carry):
-        k = j // 2
-
-        @pl.when(lax.rem(j, 2) == 0)
-        def _():
-            kv_tick(k + early)
-
-        s = jnp.where(lax.rem(j, 2) == 0, wrap(me - 1 - k), wrap(me + 1 + k))
+        direction = first + lax.rem(j, 2) * (second - first)
+        kv_tick(direction, j // 2 + early)
+        s = rs_chunk(direction, j // 2)
 
         def unit(u, c):
             qb, kb = unit_blocks(s, u)
@@ -182,11 +178,12 @@
 
     lax.fori_loop(0, n - 1, forward_step, 0)
 
-    for direction, steps in ((0, steps_right), (1, steps_left)):
+    for direction in (0, 1):
         def drain(t, c, direction=direction):
             kv_copy(direction, t).wait_send()
             return c
-        lax.fori_loop(0, steps, drain, 0)
+
+        lax.fori_loop(0, kv_steps(direction), drain, 0)
 
     for b in range(2):
         for h in range(heads):
@@ -202,11 +199,10 @@
 
     eh = embed // 2
 
-    def wo_part(t):
-        for direction in (0, 1):
-            c = rs_chunk(direction, t)
-            at = pl.ds(pl.multiple_of(c * mc, mc), mc)
-            part_o[direction] = dot(o_cols[direction * eh:(direction + 1) * eh, :], dy[:, at])
+    def wo_part(direction, t):
+        at = pl.ds(pl.multiple_of(rs_chunk(direction, t) * mc, mc), mc)
+        rows = pl.ds(pl.multiple_of(direction * eh, eh), eh)
+        part_o[direction] = dot(o_cols[rows, :], dy[:, at])
 
     def ro_copy(direction, t):
         c = rs_chunk(direction, t)
@@ -217,17 +213,17 @@
         for direction in (0, 1):
             copy(direction, t).wait_send()
 
-    def ro_tick(t):
-        for direction in (0, 1):
-            c = rs_chunk(direction, t)
-            ro_copy(direction, t - 1).wait_recv()
-            slot_o[direction, c] = slot_o[direction, c] + part_o[direction]
-
-    wo_part(0)
-    for direction in (0, 1):
+    def ro_tick(direction, t):
+        c = rs_chunk(direction, t)
+        ro_copy(direction, t - 1).wait_recv()
+        slot_o[direction, c] = slot_o[direction, c] + part_o[direction]
+
+    for direction in order:
+        wo_part(direction, 0)
         slot_o[direction, rs_chunk(direction, 0)] = part_o[direction]
         ro_copy(direction, 0).start()
-    wo_part(1)
+    for direction in order:
+        wo_part(direction, 1)
 
     part_kv0 = 0
     slot_kv0 = 2 * n * tok
@@ -274,17 +270,18 @@
         def _():
             wait_sends(ro_copy, j - 2)
 
-        @pl.when(j < n - 1)
-        def _():
-            ro_tick(j)
-            for direction in (0, 1):
-                ro_copy(direction, j).start()
-            wo_part(j + 1)
-
         zero_block(s, 0)
         zero_block(s, 1)
 
         def unit(u, c):
+            direction = first + u * (second - first)
+
+            @pl.when(j < n - 1)
+            def _():
+                ro_tick(direction, j)
+                ro_copy(direction, j).start()
+                wo_part(direction, j + 1)
+
             qb, kb = unit_blocks(s, u)
             backward_unit(s, qb, kb, False, True)
             return c
@@ -329,19 +326,19 @@
         stage[lax.rem(i, 2)] = dot(o_rows[...], wo[:, pl.ds(pl.multiple_of(i * mc, mc), mc)]).astype(BF16)
         stage_copy(y_hbm, i).start()
 
-    for direction in (0, 1):
+    for direction in order:
         c = rs_chunk(direction, 0)
         arena[pl.ds(kv_rows(slot_kv0, direction, c), tok), :] = arena[pl.ds(kv_rows(part_kv0, direction, c), tok), :]
         rkv_copy(direction, 0).start()
-    ro_tick(n - 1)
-    for direction in (0, 1):
+    for direction in order:
+        ro_tick(direction, n - 1)
         go_copy(direction, 0).start()
         go_out(direction, 0).start()
     y_piece(0)
     y_piece(1)
 
     def second_step(t, carry):
-        for direction in (0, 1):
+        for direction in order:
             c = rs_chunk(direction, t)
             rkv_copy(direction, t - 1).wait_recv()
             arena[pl.ds(kv_rows(slot_kv0, direction, c), tok), :] = rkv_add(direction, c)
@@ -351,7 +348,7 @@
         def _():
             wait_sends(ro_copy, n - 4 + t)
 
-        for direction in (0, 1):
+        for direction in order:
             go_copy(direction, t - 1).wait_recv()
             go_copy(direction, t).start()
             go_out(direction, t).start()
@@ -374,7 +371,7 @@
         return c
 
     lax.fori_loop(0, n - 1, drain_kv, 0)
-    for device in target:
+    for device in (left, right):
         pl.semaphore_signal(ready_sem, inc=1, device_id={"cp": device}, device_id_type=MESH)
 
     wrow = me_half * (heads + 2)
@@ -382,30 +379,28 @@
     def w_rows(direction, c):
         return pl.multiple_of((direction * n + c) * wrow, wrow)
 
-    def w_part(t):
-        for direction in (0, 1):
-            c = rs_chunk(direction, t)
-            at = pl.ds(pl.multiple_of(c * mc + direction * me_half, me_half), me_half)
-            x_cols[...] = x[:, at].T
-            for g in range((embed + kvw) // 256):
-                block = dot(x_cols[...], dqkv[:, g * 256:(g + 1) * 256])
-                for i in range(per):
-                    h = g * per + i
-                    piece = block[:, i * hd:(i + 1) * hd]
-                    if h < heads:
-                        part_w[direction, pl.ds(h, me_half, stride=heads), :] = piece
-                    else:
-                        part_w[direction, pl.ds(h * me_half, me_half), :] = piece
+    def w_part(direction, t):
+        c = rs_chunk(direction, t)
+        at = pl.ds(pl.multiple_of(c * mc + direction * me_half, me_half), me_half)
+        x_cols[...] = x[:, at].T
+        for g in range((embed + kvw) // 256):
+            block = dot(x_cols[...], dqkv[:, g * 256:(g + 1) * 256])
+            for i in range(per):
+                h = g * per + i
+                piece = block[:, i * hd:(i + 1) * hd]
+                if h < heads:
+                    part_w[direction, pl.ds(h, me_half, stride=heads), :] = piece
+                else:
+                    part_w[direction, pl.ds(h * me_half, me_half), :] = piece
 
     def rw_copy(direction, t):
         rows = pl.ds(w_rows(direction, rs_chunk(direction, t)), wrow)
         return rcopy(arena.at[rows], arena.at[rows], rw_send.at[direction, t], rw_recv.at[direction, t], direction)
 
-    def rw_tick(t):
-        for direction in (0, 1):
-            rows = pl.ds(w_rows(direction, rs_chunk(direction, t)), wrow)
-            rw_copy(direction, t - 1).wait_recv()
-            arena[rows, :] = arena[rows, :] + part_w[direction]
+    def rw_tick(direction, t):
+        rows = pl.ds(w_rows(direction, rs_chunk(direction, t)), wrow)
+        rw_copy(direction, t - 1).wait_recv()
+        arena[rows, :] = arena[rows, :] + part_w[direction]
 
     def gw_copy(direction, t):
         rows = pl.ds(w_rows(direction, ag_chunk(direction, t)), wrow)
@@ -424,12 +419,15 @@
             for k, (dst, skip, rows) in enumerate(((gq_hbm, 0, heads), (gk_hbm, heads, 1), (gv_hbm, heads + 1, 1)))
         ]
 
-    w_part(0)
+    w_part(first, 0)
     pl.semaphore_wait(ready_sem, 2)
-    for direction in (0, 1):
+    for direction in order:
+        if direction is second:
+            w_part(second, 0)
         arena[pl.ds(w_rows(direction, rs_chunk(direction, 0)), wrow), :] = part_w[direction]
         rw_copy(direction, 0).start()
-    w_part(1)
+    for direction in order:
+        w_part(direction, 1)
 
     for direction in (0, 1):
         go_copy(direction, n - 2).wait_recv()
@@ -442,10 +440,10 @@
         def _():
             wait_sends(rw_copy, t - 2)
 
-        rw_tick(t)
-        for direction in (0, 1):
+        for direction in order:
+            rw_tick(direction, t)
             rw_copy(direction, t).start()
-        w_part(t + 1)
+            w_part(direction, t + 1)
         return carry
 
     lax.fori_loop(1, n - 1, third_step, 0)
@@ -455,8 +453,8 @@
         stage[lax.rem(i, 2)] = dot_nt(dqkv[...], wqkv[at, :]).astype(BF16)
         stage_copy(dx_hbm, i).start()
 
-    rw_tick(n - 1)
-    for direction in (0, 1):
+    for direction in order:
+        rw_tick(direction, n - 1)
         gw_copy(direction, 0).start()
         for copy in gw_out(direction, 0):
             copy.start()
@@ -468,7 +466,7 @@
         def _():
             wait_sends(rw_copy, n - 4 + t)
 
-        for direction in (0, 1):
+        for direction in order:
             gw_copy(direction, t - 1).wait_recv()
             gw_copy(direction, t).start()
             for copy in gw_out(direction, t):

time: 448 us -> 368 us (0.82)
  Pallas kernels: 420 us -> 341 us
    pallas_call x1, Pallas kernels: 420 us -> 341 us  [device_layer(): pl.pallas_call(functools.partial(layer_kernel, n, heads), name='attention...]
where the time goes in v2:
time: 368 us
  Pallas kernels  341 us (93%)
  local copies, waits for them, and re-layouts  26.8 us (7%)
    pallas_call x1, Pallas kernels, device_layer(): pl.pallas_call(functools.partial(layer_kernel, n, heads), name='attention...  341 us
    unnamed x17, local copies, waits for them, and re-layouts  26.8 us

profile of v2, /device:TPU:21, one launch (start us, length us, event | category | flops | bytes accessed | tf_op | source)
XLA Modules:
  0.0 368.3 jit_solution(3349072317630384798)
XLA Ops:
  0.6 4.9 %copy.16 = bf16[512,8,4,128]{3,1,2,0:T(8,128)(2,1)} copy(bf16[512,8,4,128]{3,2,1,0:T(4,128)(2,1)} %bitcast.20) | data formatting | bytes 8388608
  5.6 340.9 %attention_layer.1 = (bf16[512,4096]{1,0:T(8,128)(2,1)}, bf16[512,4096]{1,0:T(8,128)(2,1)}, f32[16384,128]{1,0:T(8,128)}, f32[4096,128]{1,0:T(8,128)}, f32[4096,128]{1,0:T(8,128)}, /*index=5*/f32[512,4096]{1,0:T(8,128)}) custom-call(bf16[512,4096]{1,0:T(8,128)(2,1)} %x_hbm.1, bf16[512,4096]{1,0:T(8,128)(2,1)} %dy_hbm.1, bf16[4096,512]{1,0:T(8,128)(2,1)} %bitcast.15, ...), custom_call_target="tpu_custom_call" | custom-call | tf_op jit(solution)/shard_map/attention_layer/pallas_call | solution.py:523
  346.4 0.0 copy-start
  346.4 5.0 %copy.23 = bf16[512,4096]{1,0:T(8,128)(2,1)} copy(bf16[512,4096]{1,0:T(8,128)(2,1)} %get-tuple-element.30) | data formatting | bytes 8388608
  351.4 0.0 slice-start
  351.4 4.9 %copy.24 = bf16[512,4096]{1,0:T(8,128)(2,1)} copy(bf16[512,4096]{1,0:T(8,128)(2,1)} %get-tuple-element.31) | data formatting | bytes 8388608
  356.3 0.0 copy-done
  356.3 0.0 copy-start.2
  356.3 0.0 slice-start.1
  356.3 4.3 %copy.25 = f32[4096,4,128]{2,1,0:T(4,128)} copy(f32[4096,4,128]{2,1,0:T(4,128)S(1)} %bitcast.19) | data formatting | bytes 16777216
  360.6 0.0 copy-done.2
  360.6 0.0 copy-start.1
  360.6 1.3 copy.26
  361.9 1.7 copy-done.1
  363.6 1.3 copy.27
  364.9 0.0 slice-done
  364.9 0.0 slice-done.1
  364.9 3.4 copy.28
  (1 shorter events, 0.0 us)
Async XLA Ops:
  346.4 9.9 %copy-start = (f32[16384,128]{1,0:T(8,128)S(1)}, f32[16384,128]{1,0:T(8,128)}, u32[]{:S(2)}) copy-start(f32[16384,128]{1,0:T(8,128)} %get-tuple-element.14) | copy-start | bytes 25165828
  351.4 13.5 %slice-start = ((s8[8388608]{0:T(1024)(128)(4,1)}), s8[4194304]{0:T(1024)(128)(4,1)S(1)}, s32[]{:S(2)}) async-start(s8[8388608]{0:T(1024)(128)(4,1)} %bitcast.16), calls=%async_computation | async-start | bytes 8388608
  356.3 4.3 %copy-start.2 = (f32[4096,128]{1,0:T(8,128)S(1)}, f32[4096,128]{1,0:T(8,128)}, u32[]{:S(2)}) copy-start(f32[4096,128]{1,0:T(8,128)} %get-tuple-element.15) | copy-start | bytes 6291460
  356.3 8.6 %slice-start.1 = ((s8[8388608]{0:T(1024)(128)(4,1)}), s8[4194304]{0:T(1024)(128)(4,1)S(1)}, s32[]{:S(2)}) async-start(s8[8388608]{0:T(1024)(128)(4,1)} %bitcast.16), calls=%async_computation.1 | async-start | bytes 8388608
  360.6 3.0 copy-start.1

commit v3 on v2

--- a/solution.py
+++ b/solution.py
@@ -26,9 +26,9 @@
     n, heads, x_hbm, dy_hbm, wq_hbm, wk_hbm, wv_hbm, wo_hbm,
     y_hbm, dx_hbm, gq_hbm, gk_hbm, gv_hbm, go_hbm,
     x, dy, wqkv, wo, kv, q_rows, q_cols, do_rows, do_cols, o_rows, o_cols,
-    acc, m_state, l_state, delta, dqkv, p_cols, ds_cols, slot_o, part_o, arena, part_w, x_cols, stage,
+    acc, m_state, l_state, delta, dqkv, slot_o, part_o, arena, part_w, x_cols, stage, extra_ob, gift_ob, extra_kvb, extra_wb, gift_wb,
     in_sem, kv_send, kv_recv, ro_send, ro_recv, go_send, go_recv, rkv_send, rkv_recv,
-    rw_send, rw_recv, gw_send, gw_recv, out_o_sem, out_w_sem, stage_sem, ready_sem,
+    rw_send, rw_recv, gw_send, gw_recv, extra_send, extra_recv, out_o_sem, out_w_sem, stage_sem, ready_sem,
 ):
     tok, width = x.shape
     half = tok // 2
@@ -70,7 +70,7 @@
         pltpu.make_async_copy(dy_hbm, dy, in_sem.at[4]),
         pltpu.make_async_copy(wo_hbm, wo, in_sem.at[5]),
     ]
-    for load in loads:
+    for load in loads[:3]:
         load.start()
 
     barrier = pltpu.get_barrier_semaphore()
@@ -79,6 +79,8 @@
 
     for load in loads[:3]:
         load.wait()
+    for load in loads[3:]:
+        load.start()
 
     kv[me] = dot(x[...], wqkv[:, embed:]).astype(BF16)
     pl.semaphore_wait(barrier, 2)
@@ -124,37 +126,30 @@
     for g in range(embed // 256):
         project_q(g)
         kv_tick(order[g % 2], g // 2)
-    loads[4].wait()
-    loads[5].wait()
-    for g in range(embed // 256):
-        project_do(g)
-        kv_tick(order[g % 2], embed // 512 + g // 2)
-    early = embed // 256
+    early = embed // 512
 
     m_state[...] = jnp.full(m_state.shape, -jnp.inf, F32)
     l_state[...] = jnp.zeros(l_state.shape, F32)
     acc[...] = jnp.zeros(acc.shape, F32)
 
     def diagonal():
-        key_id = lax.broadcasted_iota(jnp.int32, (half, half), 0)
-        query_id = lax.broadcasted_iota(jnp.int32, (half, half), 1)
+        key_id = lax.broadcasted_iota(jnp.int32, (half, cols), 0)
+        query_id = lax.rem(lax.broadcasted_iota(jnp.int32, (half, cols), 1), half)
         return key_id <= query_id
 
     def forward_unit(s, qb, kb, masked):
         keys = kv[s, pl.ds(kb * half, half), :hd]
         values_t = kv[s, pl.ds(kb * half, half), hd:].T
-        for h in range(heads):
-            lanes = slice(h * half, (h + 1) * half)
-            sc = dot(keys, q_cols[qb, :, lanes])
-            if masked:
-                sc = jnp.where(diagonal(), sc, -jnp.inf)
-            old = m_state[qb, :, lanes]
-            new = jnp.maximum(old, jnp.max(sc, axis=0, keepdims=True) * scale2)
-            fade = jnp.exp2(old - new)
-            p = jnp.exp2(sc * scale2 - new)
-            l_state[qb, :, lanes] = l_state[qb, :, lanes] * fade + jnp.sum(p, axis=0, keepdims=True)
-            m_state[qb, :, lanes] = new
-            acc[qb, :, lanes] = acc[qb, :, lanes] * fade + dot(values_t, p.astype(BF16))
+        sc = dot(keys, q_cols[qb])
+        if masked:
+            sc = jnp.where(diagonal(), sc, -jnp.inf)
+        old = m_state[qb]
+        new = jnp.maximum(old, jnp.max(sc, axis=0, keepdims=True) * scale2)
+        fade = jnp.exp2(old - new)
+        p = jnp.exp2(sc * scale2 - new)
+        l_state[qb] = l_state[qb] * fade + jnp.sum(p, axis=0, keepdims=True)
+        m_state[qb] = new
+        acc[qb] = acc[qb] * fade + dot(values_t, p.astype(BF16))
 
     forward_unit(me, 1, 0, False)
     forward_unit(me, 0, 0, True)
@@ -192,9 +187,6 @@
             out = (acc[b, :, lanes] / total).astype(BF16)
             o_cols[h * hd:(h + 1) * hd, b * half:(b + 1) * half] = out
             o_rows[b * half:(b + 1) * half, h * hd:(h + 1) * hd] = out.T
-            delta[b, :, lanes] = jnp.sum(
-                out.astype(F32) * do_cols[b, :, lanes].astype(F32), axis=0, keepdims=True
-            )
             m_state[b, :, lanes] = m_state[b, :, lanes] + jnp.log(total) * math.log2(math.e)
 
     eh = embed // 2
@@ -210,20 +202,58 @@
                      ro_send.at[direction, t], ro_recv.at[direction, t], direction)
 
     def wait_sends(copy, t):
-        for direction in (0, 1):
-            copy(direction, t).wait_send()
+        copy(second, t).wait_send()
+
+        @pl.when(t > 0)
+        def _():
+            copy(first, t).wait_send()
 
     def ro_tick(direction, t):
         c = rs_chunk(direction, t)
         ro_copy(direction, t - 1).wait_recv()
         slot_o[direction, c] = slot_o[direction, c] + part_o[direction]
 
+    def extra_copy(src, dst, k):
+        return rcopy(src, dst, extra_send.at[k], extra_recv.at[k], second)
+
+    def extra_o():
+        return extra_copy(slot_o.at[first, rs_chunk(first, 0)], extra_ob, 0)
+
+    def gift_o():
+        return extra_copy(slot_o.at[first, me], gift_ob, 1)
+
+    loads[4].wait()
+    wo_part(first, 0)
+    slot_o[first, rs_chunk(first, 0)] = part_o[first]
+    extra_o().start()
+    wo_part(second, 0)
+    slot_o[second, rs_chunk(second, 0)] = part_o[second]
+    ro_copy(second, 0).start()
+    wo_part(second, 1)
+    slot_o[second, rs_chunk(second, 1)] = part_o[second]
+    wo_part(first, 1)
+    ro_tick(first, 1)
+    ro_copy(first, 1).start()
+    ro_copy(second, 1).start()
     for direction in order:
-        wo_part(direction, 0)
-        slot_o[direction, rs_chunk(direction, 0)] = part_o[direction]
-        ro_copy(direction, 0).start()
-    for direction in order:
-        wo_part(direction, 1)
+        wo_part(direction, 2)
+
+    loads[5].wait()
+    for g in range(embed // 256):
+        project_do(g)
+        if g == 0:
+            ro_tick(first, 2)
+            ro_copy(first, 2).start()
+            wo_part(first, 3)
+        if g == 1:
+            ro_tick(second, 2)
+            ro_copy(second, 2).start()
+            wo_part(second, 3)
+    for b in range(2):
+        for h in range(heads):
+            lanes = slice(h * half, (h + 1) * half)
+            out = o_cols[h * hd:(h + 1) * hd, b * half:(b + 1) * half].astype(F32)
+            delta[b, :, lanes] = jnp.sum(out * do_cols[b, :, lanes].astype(F32), axis=0, keepdims=True)
 
     part_kv0 = 0
     slot_kv0 = 2 * n * tok
@@ -236,22 +266,17 @@
     def backward_unit(s, qb, kb, masked, add):
         keys = kv[s, pl.ds(kb * half, half), :hd]
         values = kv[s, pl.ds(kb * half, half), hd:]
-        keys_t = keys.T
-        for h in range(heads):
-            lanes = slice(h * half, (h + 1) * half)
-            sc = dot(keys, q_cols[qb, :, lanes])
-            p = jnp.exp2(sc * scale2 - m_state[qb, :, lanes])
-            if masked:
-                p = jnp.where(diagonal(), p, 0.0)
-            p = p.astype(BF16)
-            p_cols[:, lanes] = p
-            dp = dot(values, do_cols[qb, :, lanes])
-            ds = (p.astype(F32) * (dp - delta[qb, :, lanes])).astype(BF16)
-            ds_cols[:, lanes] = ds
-            acc[qb, :, lanes] = acc[qb, :, lanes] + dot(keys_t, ds)
-        for direction, lhs, rhs in ((0, ds_cols, q_rows), (1, p_cols, do_rows)):
+        sc = dot(keys, q_cols[qb])
+        p = jnp.exp2(sc * scale2 - m_state[qb])
+        if masked:
+            p = jnp.where(diagonal(), p, 0.0)
+        p = p.astype(BF16)
+        dp = dot(values, do_cols[qb])
+        ds = (p.astype(F32) * (dp - delta[qb])).astype(BF16)
+        acc[qb] = acc[qb] + dot(keys.T, ds)
+        for direction, lhs, rhs in ((0, ds, q_rows), (1, p, do_rows)):
             rows = pl.ds(pl.multiple_of(kv_rows(part_kv0, direction, s) + kb * half, half), half)
-            g = dot(lhs[...], rhs[qb])
+            g = dot(lhs, rhs[qb])
             arena[rows, :] = arena[rows, :] + g if add else g
 
     def zero_block(s, kb):
@@ -259,6 +284,8 @@
             rows = pl.ds(pl.multiple_of(kv_rows(part_kv0, direction, s) + kb * half, half), half)
             arena[rows, :] = jnp.zeros((half, hd), F32)
 
+    wait_sends(ro_copy, 0)
+    extra_o().wait_send()
     backward_unit(me, 1, 0, False, False)
     backward_unit(me, 0, 0, True, True)
     backward_unit(me, 1, 1, True, False)
@@ -266,9 +293,11 @@
     def backward_step(j, carry):
         s = wrap(me + j)
 
-        @pl.when(jnp.logical_and(j >= 2, j < n - 1))
+        t = j + 2
+
+        @pl.when(t < n - 1)
         def _():
-            wait_sends(ro_copy, j - 2)
+            wait_sends(ro_copy, t - 2)
 
         zero_block(s, 0)
         zero_block(s, 1)
@@ -276,11 +305,11 @@
         def unit(u, c):
             direction = first + u * (second - first)
 
-            @pl.when(j < n - 1)
+            @pl.when(t < n - 1)
             def _():
-                ro_tick(direction, j)
-                ro_copy(direction, j).start()
-                wo_part(direction, j + 1)
+                ro_tick(direction, t)
+                ro_copy(direction, t).start()
+                wo_part(direction, t + 1)
 
             qb, kb = unit_blocks(s, u)
             backward_unit(s, qb, kb, False, True)
@@ -326,23 +355,44 @@
         stage[lax.rem(i, 2)] = dot(o_rows[...], wo[:, pl.ds(pl.multiple_of(i * mc, mc), mc)]).astype(BF16)
         stage_copy(y_hbm, i).start()
 
+    def extra_kv():
+        return extra_copy(arena.at[pl.ds(kv_rows(part_kv0, first, rs_chunk(first, 0)), tok)], extra_kvb, 2)
+
+    extra_kv().start()
+    for t in (0, 1):
+        c = rs_chunk(second, t)
+        arena[pl.ds(kv_rows(slot_kv0, second, c), tok), :] = arena[pl.ds(kv_rows(part_kv0, second, c), tok), :]
+        rkv_copy(second, t).start()
+    c = rs_chunk(first, 1)
+    rkv_copy(first, 0).wait_recv()
+    arena[pl.ds(kv_rows(slot_kv0, first, c), tok), :] = rkv_add(first, c)
+    rkv_copy(first, 1).start()
+    ro_tick(first, n - 1)
+    go_copy(first, 0).start()
+    gift_o().start()
+    extra_o().wait_recv()
+    part_o[second] = part_o[second] + extra_ob[...]
+    ro_tick(second, n - 1)
+    go_copy(second, 0).start()
     for direction in order:
-        c = rs_chunk(direction, 0)
-        arena[pl.ds(kv_rows(slot_kv0, direction, c), tok), :] = arena[pl.ds(kv_rows(part_kv0, direction, c), tok), :]
-        rkv_copy(direction, 0).start()
-    for direction in order:
-        ro_tick(direction, n - 1)
-        go_copy(direction, 0).start()
         go_out(direction, 0).start()
     y_piece(0)
     y_piece(1)
 
+    def ag_send(copy, direction, t):
+        @pl.when(jnp.logical_or(t < n - 2, direction == second))
+        def _():
+            copy(direction, t).start()
+
     def second_step(t, carry):
+        u = t + 1
         for direction in order:
-            c = rs_chunk(direction, t)
-            rkv_copy(direction, t - 1).wait_recv()
-            arena[pl.ds(kv_rows(slot_kv0, direction, c), tok), :] = rkv_add(direction, c)
-            rkv_copy(direction, t).start()
+            @pl.when(u < n - 1)
+            def _(direction=direction):
+                c = rs_chunk(direction, u)
+                rkv_copy(direction, u - 1).wait_recv()
+                arena[pl.ds(kv_rows(slot_kv0, direction, c), tok), :] = rkv_add(direction, c)
+                rkv_copy(direction, u).start()
 
         @pl.when(t <= 2)
         def _():
@@ -350,7 +400,7 @@
 
         for direction in order:
             go_copy(direction, t - 1).wait_recv()
-            go_copy(direction, t).start()
+            ag_send(go_copy, direction, t)
             go_out(direction, t).start()
         stage_copy(y_hbm, t - 1).wait()
         y_piece(t + 1)
@@ -358,19 +408,23 @@
 
     lax.fori_loop(1, n - 1, second_step, 0)
 
+    extra_kv().wait_recv()
+    mine = pl.ds(kv_rows(slot_kv0, second, me), tok)
+    rkv_copy(second, n - 2).wait_recv()
+    arena[mine, :] = arena[mine, :] + extra_kvb[...]
+    rkv_copy(first, n - 2).wait_recv()
     for direction in (0, 1):
-        rkv_copy(direction, n - 2).wait_recv()
         g = rkv_add(direction, me)
         if direction == 0:
             g = g * scale
         dqkv[:, embed + direction * hd:embed + (direction + 1) * hd] = g.astype(BF16)
 
     def drain_kv(t, c):
-        for direction in (0, 1):
-            rkv_copy(direction, t).wait_send()
+        wait_sends(rkv_copy, t)
         return c
 
     lax.fori_loop(0, n - 1, drain_kv, 0)
+    extra_kv().wait_send()
     for device in (left, right):
         pl.semaphore_signal(ready_sem, inc=1, device_id={"cp": device}, device_id_type=MESH)
 
@@ -406,56 +460,77 @@
         rows = pl.ds(w_rows(direction, ag_chunk(direction, t)), wrow)
         return rcopy(arena.at[rows], arena.at[rows], gw_send.at[direction, t], gw_recv.at[direction, t], direction)
 
-    def gw_out(direction, t):
+    def gw_out(direction, t, src=arena):
         c = ag_chunk(direction, t)
-        row = w_rows(direction, c)
-        first = c * mc + direction * me_half
+        row = w_rows(direction, c) if src is arena else 0
+        start = c * mc + direction * me_half
         return [
             pltpu.make_async_copy(
-                arena.at[pl.ds(row + skip * me_half, rows * me_half)],
-                dst.at[pl.ds(pl.multiple_of(first * rows, me_half), rows * me_half)],
+                src.at[pl.ds(row + skip * me_half, rows * me_half)],
+                dst.at[pl.ds(pl.multiple_of(start * rows, me_half), rows * me_half)],
                 out_w_sem.at[direction, t, k],
             )
             for k, (dst, skip, rows) in enumerate(((gq_hbm, 0, heads), (gk_hbm, heads, 1), (gv_hbm, heads + 1, 1)))
         ]
 
+    def extra_w():
+        return extra_copy(arena.at[pl.ds(w_rows(first, rs_chunk(first, 0)), wrow)], extra_wb, 3)
+
+    def gift_w():
+        return extra_copy(arena.at[pl.ds(w_rows(first, me), wrow)], gift_wb, 4)
+
+    w_part(second, 0)
+    pl.semaphore_wait(ready_sem, 2)
+    arena[pl.ds(w_rows(second, rs_chunk(second, 0)), wrow), :] = part_w[second]
+    rw_copy(second, 0).start()
+    w_part(first, 1)
+    rw_tick(first, 1)
+    rw_copy(first, 1).start()
     w_part(first, 0)
-    pl.semaphore_wait(ready_sem, 2)
+    arena[pl.ds(w_rows(first, rs_chunk(first, 0)), wrow), :] = part_w[first]
+    extra_w().start()
+    w_part(second, 1)
+    arena[pl.ds(w_rows(second, rs_chunk(second, 1)), wrow), :] = part_w[second]
+    rw_copy(second, 1).start()
     for direction in order:
-        if direction is second:
-            w_part(second, 0)
-        arena[pl.ds(w_rows(direction, rs_chunk(direction, 0)), wrow), :] = part_w[direction]
-        rw_copy(direction, 0).start()
-    for direction in order:
-        w_part(direction, 1)
-
-    for direction in (0, 1):
-        go_copy(direction, n - 2).wait_recv()
-        go_out(direction, n - 1).start()
+        w_part(direction, 2)
+
+    def last_o():
+        at = pl.ds(pl.multiple_of(ag_chunk(second, n - 1) * mc, mc), mc)
+        rows = pl.ds(pl.multiple_of(second * eh, eh), eh)
+        return pltpu.make_async_copy(gift_ob, go_hbm.at[rows, at], out_o_sem.at[second, n - 1])
+
+    go_copy(first, n - 2).wait_recv()
+    go_out(first, n - 1).start()
+    gift_o().wait_recv()
+    last_o().start()
     stage_copy(y_hbm, n - 2).wait()
     stage_copy(y_hbm, n - 1).wait()
 
     def third_step(t, carry):
-        @pl.when(t >= 2)
-        def _():
-            wait_sends(rw_copy, t - 2)
-
+        wait_sends(rw_copy, t - 2)
         for direction in order:
             rw_tick(direction, t)
             rw_copy(direction, t).start()
             w_part(direction, t + 1)
         return carry
 
-    lax.fori_loop(1, n - 1, third_step, 0)
+    extra_w().wait_send()
+    lax.fori_loop(2, n - 1, third_step, 0)
 
     def dx_piece(i):
         at = pl.ds(pl.multiple_of(i * mc, mc), mc)
         stage[lax.rem(i, 2)] = dot_nt(dqkv[...], wqkv[at, :]).astype(BF16)
         stage_copy(dx_hbm, i).start()
 
+    rw_tick(first, n - 1)
+    gw_copy(first, 0).start()
+    gift_w().start()
+    extra_w().wait_recv()
+    part_w[second] = part_w[second] + extra_wb[...]
+    rw_tick(second, n - 1)
+    gw_copy(second, 0).start()
     for direction in order:
-        rw_tick(direction, n - 1)
-        gw_copy(direction, 0).start()
         for copy in gw_out(direction, 0):
             copy.start()
     dx_piece(0)
@@ -468,7 +543,7 @@
 
         for direction in order:
             gw_copy(direction, t - 1).wait_recv()
-            gw_copy(direction, t).start()
+            ag_send(gw_copy, direction, t)
             for copy in gw_out(direction, t):
                 copy.start()
         stage_copy(dx_hbm, t - 1).wait()
@@ -480,27 +555,30 @@
     stage_copy(dx_hbm, n - 2).wait()
     stage_copy(dx_hbm, n - 1).wait()
 
+    gw_copy(first, n - 2).wait_recv()
+    gift_w().wait_recv()
+    for copy in gw_out(first, n - 1) + gw_out(second, n - 1, gift_wb):
+        copy.start()
+
     def drain_all(t, c):
+        for copy in (go_copy, gw_copy):
+            copy(second, t).wait_send()
+
+            @pl.when(t < n - 2)
+            def _(copy=copy):
+                copy(first, t).wait_send()
+
         for direction in (0, 1):
-            go_copy(direction, t).wait_send()
-            gw_copy(direction, t).wait_send()
             go_out(direction, t).wait()
-        return c
-
-    lax.fori_loop(0, n - 1, drain_all, 0)
-    for direction in (0, 1):
-        go_out(direction, n - 1).wait()
-        gw_copy(direction, n - 2).wait_recv()
-        for copy in gw_out(direction, n - 1):
-            copy.start()
-
-    def drain_out(t, c):
-        for direction in (0, 1):
             for copy in gw_out(direction, t):
                 copy.wait()
         return c
 
-    lax.fori_loop(0, n, drain_out, 0)
+    lax.fori_loop(0, n - 1, drain_all, 0)
+    for copy in [go_out(first, n - 1), last_o()] + gw_out(first, n - 1) + gw_out(second, n - 1, gift_wb):
+        copy.wait()
+    for copy in (gift_o, gift_w):
+        copy().wait_send()
 
 
 def solution(mesh):
@@ -550,18 +628,21 @@
                 pltpu.VMEM((2, 1, cols), F32),
                 pltpu.VMEM((2, 1, cols), F32),
                 pltpu.VMEM((tok, embed + kvw), BF16),
-                pltpu.VMEM((half, cols), BF16),
-                pltpu.VMEM((half, cols), BF16),
                 pltpu.VMEM((2, n, embed // 2, mc), F32),
                 pltpu.VMEM((2, embed // 2, mc), F32),
                 pltpu.VMEM((max(4 * n * tok, 2 * n * wrow), hd), F32),
                 pltpu.VMEM((2, wrow, hd), F32),
                 pltpu.VMEM((mc // 2, tok), BF16),
                 pltpu.VMEM((2, tok, mc), BF16),
+                pltpu.VMEM((embed // 2, mc), F32),
+                pltpu.VMEM((embed // 2, mc), F32),
+                pltpu.VMEM((tok, hd), F32),
+                pltpu.VMEM((wrow, hd), F32),
+                pltpu.VMEM((wrow, hd), F32),
                 dma(6),
                 dma(2, n // 2), dma(2, n // 2),
                 ring, ring, ring, ring, ring, ring, ring, ring, ring, ring,
-                dma(2, n), dma(2, n, 3), dma(2),
+                dma(5), dma(5), dma(2, n), dma(2, n, 3), dma(2),
                 pltpu.SemaphoreType.REGULAR,
             ],
             compiler_params=pltpu.CompilerParams(

time: 368 us -> 342 us (0.929)
  Pallas kernels: 341 us -> 315 us
    pallas_call x1, Pallas kernels: 341 us -> 315 us  [device_layer(): pl.pallas_call(functools.partial(layer_kernel, n, heads), name='attention...]
where the time goes in v3:
time: 342 us
  Pallas kernels  315 us (92%)
  local copies, waits for them, and re-layouts  26.8 us (8%)
    pallas_call x1, Pallas kernels, device_layer(): pl.pallas_call(functools.partial(layer_kernel, n, heads), name='attention...  315 us
    unnamed x17, local copies, waits for them, and re-layouts  26.8 us

profile of v3, /device:TPU:21, one launch (start us, length us, event | category | flops | bytes accessed | tf_op | source)
XLA Modules:
  0.0 342.1 jit_solution(16721241177500447841)
XLA Ops:
  0.6 4.9 %copy.16 = bf16[512,8,4,128]{3,1,2,0:T(8,128)(2,1)} copy(bf16[512,8,4,128]{3,2,1,0:T(4,128)(2,1)} %bitcast.20) | data formatting | bytes 8388608
  5.6 314.6 %attention_layer.1 = (bf16[512,4096]{1,0:T(8,128)(2,1)}, bf16[512,4096]{1,0:T(8,128)(2,1)}, f32[16384,128]{1,0:T(8,128)}, f32[4096,128]{1,0:T(8,128)}, f32[4096,128]{1,0:T(8,128)}, /*index=5*/f32[512,4096]{1,0:T(8,128)}) custom-call(bf16[512,4096]{1,0:T(8,128)(2,1)} %x_hbm.1, bf16[512,4096]{1,0:T(8,128)(2,1)} %dy_hbm.1, bf16[4096,512]{1,0:T(8,128)(2,1)} %bitcast.15, ...), custom_call_target="tpu_custom_call" | custom-call | tf_op jit(solution)/shard_map/attention_layer/pallas_call | solution.py:601
  320.2 0.0 copy-start
  320.2 5.0 %copy.23 = bf16[512,4096]{1,0:T(8,128)(2,1)} copy(bf16[512,4096]{1,0:T(8,128)(2,1)} %get-tuple-element.30) | data formatting | bytes 8388608
  325.2 0.0 slice-start
  325.2 4.9 %copy.24 = bf16[512,4096]{1,0:T(8,128)(2,1)} copy(bf16[512,4096]{1,0:T(8,128)(2,1)} %get-tuple-element.31) | data formatting | bytes 8388608
  330.1 0.0 copy-done
  330.1 0.0 copy-start.2
  330.1 0.0 slice-start.1
  330.1 4.3 %copy.25 = f32[4096,4,128]{2,1,0:T(4,128)} copy(f32[4096,4,128]{2,1,0:T(4,128)S(1)} %bitcast.19) | data formatting | bytes 16777216
  334.3 0.0 copy-done.2
  334.3 0.0 copy-start.1
  334.3 1.3 copy.26
  335.7 1.7 copy-done.1
  337.3 1.3 copy.27
  338.7 0.0 slice-done
  338.7 0.0 slice-done.1
  338.7 3.4 copy.28
  (1 shorter events, 0.0 us)
Async XLA Ops:
  320.2 9.9 %copy-start = (f32[16384,128]{1,0:T(8,128)S(1)}, f32[16384,128]{1,0:T(8,128)}, u32[]{:S(2)}) copy-start(f32[16384,128]{1,0:T(8,128)} %get-tuple-element.14) | copy-start | bytes 25165828
  325.2 13.5 %slice-start = ((s8[8388608]{0:T(1024)(128)(4,1)}), s8[4194304]{0:T(1024)(128)(4,1)S(1)}, s32[]{:S(2)}) async-start(s8[8388608]{0:T(1024)(128)(4,1)} %bitcast.16), calls=%async_computation | async-start | bytes 8388608
  330.1 4.3 %copy-start.2 = (f32[4096,128]{1,0:T(8,128)S(1)}, f32[4096,128]{1,0:T(8,128)}, u32[]{:S(2)}) copy-start(f32[4096,128]{1,0:T(8,128)} %get-tuple-element.15) | copy-start | bytes 6291460
  330.1 8.6 %slice-start.1 = ((s8[8388608]{0:T(1024)(128)(4,1)}), s8[4194304]{0:T(1024)(128)(4,1)S(1)}, s32[]{:S(2)}) async-start(s8[8388608]{0:T(1024)(128)(4,1)} %bitcast.16), calls=%async_computation.1 | async-start | bytes 8388608
  334.3 3.0 copy-start.1

commit v4 on v3

--- a/solution.py
+++ b/solution.py
@@ -12,6 +12,7 @@
 BF16 = jnp.bfloat16
 MESH = pl.DeviceIdType.MESH
 HBM = pl.BlockSpec(memory_space=pl.ANY)
+VMEM = pl.BlockSpec(memory_space=pltpu.VMEM)
 
 
 def dot(a, b):
@@ -24,11 +25,11 @@
 
 def layer_kernel(
     n, heads, x_hbm, dy_hbm, wq_hbm, wk_hbm, wv_hbm, wo_hbm,
-    y_hbm, dx_hbm, gq_hbm, gk_hbm, gv_hbm, go_hbm,
-    x, dy, wqkv, wo, kv, q_rows, q_cols, do_rows, do_cols, o_rows, o_cols,
-    acc, m_state, l_state, delta, dqkv, slot_o, part_o, arena, part_w, x_cols, stage, extra_ob, gift_ob, extra_kvb, extra_wb, gift_wb,
+    x, dy, slot_o, arena,
+    wqkv, wo, kv, q_rows, q_cols, do_rows, do_cols, o_rows, o_cols,
+    acc, m_state, l_state, delta, dqkv, part_o, part_w, x_cols, extra_ob, gift_ob, extra_kvb, extra_wb, gift_wb,
     in_sem, kv_send, kv_recv, ro_send, ro_recv, go_send, go_recv, rkv_send, rkv_recv,
-    rw_send, rw_recv, gw_send, gw_recv, extra_send, extra_recv, out_o_sem, out_w_sem, stage_sem, ready_sem,
+    rw_send, rw_recv, gw_send, gw_recv, extra_send, extra_recv, ready_sem,
 ):
     tok, width = x.shape
     half = tok // 2
@@ -191,27 +192,40 @@
 
     eh = embed // 2
 
-    def wo_part(direction, t):
+    es = eh // 2
+
+    def sub_rows(sub, size):
+        return pl.ds(pl.multiple_of(sub * size, size), size)
+
+    def wo_part(direction, t, sub):
         at = pl.ds(pl.multiple_of(rs_chunk(direction, t) * mc, mc), mc)
-        rows = pl.ds(pl.multiple_of(direction * eh, eh), eh)
-        part_o[direction] = dot(o_cols[rows, :], dy[:, at])
-
-    def ro_copy(direction, t):
+        rows = pl.ds(pl.multiple_of(direction * eh + sub * es, es), es)
+        part_o[direction, sub_rows(sub, es), :] = dot(o_cols[rows, :], dy[:, at])
+
+    def ro_copy(direction, t, sub):
+        piece = slot_o.at[direction, rs_chunk(direction, t), sub_rows(sub, es)]
+        return rcopy(piece, piece, ro_send.at[direction, t, sub], ro_recv.at[direction, t, sub], direction)
+
+    def wait_sends(copy, t):
+        for sub in (0, 1):
+            copy(second, t, sub).wait_send()
+
+            @pl.when(t > 0)
+            def _(sub=sub):
+                copy(first, t, sub).wait_send()
+
+    def ro_tick(direction, t, sub):
         c = rs_chunk(direction, t)
-        return rcopy(slot_o.at[direction, c], slot_o.at[direction, c],
-                     ro_send.at[direction, t], ro_recv.at[direction, t], direction)
-
-    def wait_sends(copy, t):
-        copy(second, t).wait_send()
-
-        @pl.when(t > 0)
-        def _():
-            copy(first, t).wait_send()
-
-    def ro_tick(direction, t):
-        c = rs_chunk(direction, t)
-        ro_copy(direction, t - 1).wait_recv()
-        slot_o[direction, c] = slot_o[direction, c] + part_o[direction]
+        rows = sub_rows(sub, es)
+        ro_copy(direction, t - 1, sub).wait_recv()
+        slot_o[direction, c, rows, :] = slot_o[direction, c, rows, :] + part_o[direction, rows, :]
+
+    def ro_step(t, sub):
+        for direction in order:
+            ro_tick(direction, t, sub)
+            ro_copy(direction, t, sub).start()
+        for direction in order:
+            wo_part(direction, t + 1, sub)
 
     def extra_copy(src, dst, k):
         return rcopy(src, dst, extra_send.at[k], extra_recv.at[k], second)
@@ -223,32 +237,31 @@
         return extra_copy(slot_o.at[first, me], gift_ob, 1)
 
     loads[4].wait()
-    wo_part(first, 0)
+    for sub in (0, 1):
+        wo_part(second, 0, sub)
+        slot_o[second, rs_chunk(second, 0), sub_rows(sub, es), :] = part_o[second, sub_rows(sub, es), :]
+        ro_copy(second, 0, sub).start()
+    for sub in (0, 1):
+        wo_part(first, 1, sub)
+        ro_tick(first, 1, sub)
+        ro_copy(first, 1, sub).start()
+    for sub in (0, 1):
+        wo_part(second, 1, sub)
+        slot_o[second, rs_chunk(second, 1), sub_rows(sub, es), :] = part_o[second, sub_rows(sub, es), :]
+        ro_copy(second, 1, sub).start()
+    for sub in (0, 1):
+        wo_part(first, 0, sub)
     slot_o[first, rs_chunk(first, 0)] = part_o[first]
     extra_o().start()
-    wo_part(second, 0)
-    slot_o[second, rs_chunk(second, 0)] = part_o[second]
-    ro_copy(second, 0).start()
-    wo_part(second, 1)
-    slot_o[second, rs_chunk(second, 1)] = part_o[second]
-    wo_part(first, 1)
-    ro_tick(first, 1)
-    ro_copy(first, 1).start()
-    ro_copy(second, 1).start()
-    for direction in order:
-        wo_part(direction, 2)
+    for sub in (0, 1):
+        for direction in order:
+            wo_part(direction, 2, sub)
 
     loads[5].wait()
     for g in range(embed // 256):
         project_do(g)
-        if g == 0:
-            ro_tick(first, 2)
-            ro_copy(first, 2).start()
-            wo_part(first, 3)
-        if g == 1:
-            ro_tick(second, 2)
-            ro_copy(second, 2).start()
-            wo_part(second, 3)
+        if g < 2:
+            ro_step(2, g)
     for b in range(2):
         for h in range(heads):
             lanes = slice(h * half, (h + 1) * half)
@@ -303,13 +316,9 @@
         zero_block(s, 1)
 
         def unit(u, c):
-            direction = first + u * (second - first)
-
             @pl.when(t < n - 1)
             def _():
-                ro_tick(direction, t)
-                ro_copy(direction, t).start()
-                wo_part(direction, t + 1)
+                ro_step(t, u)
 
             qb, kb = unit_blocks(s, u)
             backward_unit(s, qb, kb, False, True)
@@ -338,22 +347,9 @@
         return rcopy(slot_o.at[direction, c], slot_o.at[direction, c],
                      go_send.at[direction, t], go_recv.at[direction, t], direction)
 
-    def go_out(direction, t):
-        c = ag_chunk(direction, t)
-        return pltpu.make_async_copy(
-            slot_o.at[direction, c],
-            go_hbm.at[pl.ds(direction * eh, eh), pl.ds(pl.multiple_of(c * mc, mc), mc)],
-            out_o_sem.at[direction, t],
-        )
-
-    def stage_copy(dst, i):
-        return pltpu.make_async_copy(
-            stage.at[lax.rem(i, 2)], dst.at[:, pl.ds(pl.multiple_of(i * mc, mc), mc)], stage_sem.at[lax.rem(i, 2)]
-        )
-
     def y_piece(i):
-        stage[lax.rem(i, 2)] = dot(o_rows[...], wo[:, pl.ds(pl.multiple_of(i * mc, mc), mc)]).astype(BF16)
-        stage_copy(y_hbm, i).start()
+        at = pl.ds(pl.multiple_of(i * mc, mc), mc)
+        dy[:, at] = dot(o_rows[...], wo[:, at]).astype(BF16)
 
     def extra_kv():
         return extra_copy(arena.at[pl.ds(kv_rows(part_kv0, first, rs_chunk(first, 0)), tok)], extra_kvb, 2)
@@ -367,22 +363,22 @@
     rkv_copy(first, 0).wait_recv()
     arena[pl.ds(kv_rows(slot_kv0, first, c), tok), :] = rkv_add(first, c)
     rkv_copy(first, 1).start()
-    ro_tick(first, n - 1)
+    for sub in (0, 1):
+        ro_tick(first, n - 1, sub)
     go_copy(first, 0).start()
     gift_o().start()
     extra_o().wait_recv()
     part_o[second] = part_o[second] + extra_ob[...]
-    ro_tick(second, n - 1)
+    for sub in (0, 1):
+        ro_tick(second, n - 1, sub)
     go_copy(second, 0).start()
-    for direction in order:
-        go_out(direction, 0).start()
     y_piece(0)
     y_piece(1)
 
     def ag_send(copy, direction, t):
         @pl.when(jnp.logical_or(t < n - 2, direction == second))
         def _():
-            copy(direction, t).start()
+            copy.start()
 
     def second_step(t, carry):
         u = t + 1
@@ -400,9 +396,7 @@
 
         for direction in order:
             go_copy(direction, t - 1).wait_recv()
-            ag_send(go_copy, direction, t)
-            go_out(direction, t).start()
-        stage_copy(y_hbm, t - 1).wait()
+            ag_send(go_copy(direction, t), direction, t)
         y_piece(t + 1)
         return carry
 
@@ -420,7 +414,12 @@
         dqkv[:, embed + direction * hd:embed + (direction + 1) * hd] = g.astype(BF16)
 
     def drain_kv(t, c):
-        wait_sends(rkv_copy, t)
+        rkv_copy(second, t).wait_send()
+
+        @pl.when(t > 0)
+        def _():
+            rkv_copy(first, t).wait_send()
+
         return c
 
     lax.fori_loop(0, n - 1, drain_kv, 0)
@@ -447,31 +446,23 @@
                 else:
                     part_w[direction, pl.ds(h * me_half, me_half), :] = piece
 
-    def rw_copy(direction, t):
-        rows = pl.ds(w_rows(direction, rs_chunk(direction, t)), wrow)
-        return rcopy(arena.at[rows], arena.at[rows], rw_send.at[direction, t], rw_recv.at[direction, t], direction)
-
-    def rw_tick(direction, t):
-        rows = pl.ds(w_rows(direction, rs_chunk(direction, t)), wrow)
-        rw_copy(direction, t - 1).wait_recv()
-        arena[rows, :] = arena[rows, :] + part_w[direction]
-
-    def gw_copy(direction, t):
-        rows = pl.ds(w_rows(direction, ag_chunk(direction, t)), wrow)
-        return rcopy(arena.at[rows], arena.at[rows], gw_send.at[direction, t], gw_recv.at[direction, t], direction)
-
-    def gw_out(direction, t, src=arena):
-        c = ag_chunk(direction, t)
-        row = w_rows(direction, c) if src is arena else 0
-        start = c * mc + direction * me_half
-        return [
-            pltpu.make_async_copy(
-                src.at[pl.ds(row + skip * me_half, rows * me_half)],
-                dst.at[pl.ds(pl.multiple_of(start * rows, me_half), rows * me_half)],
-                out_w_sem.at[direction, t, k],
-            )
-            for k, (dst, skip, rows) in enumerate(((gq_hbm, 0, heads), (gk_hbm, heads, 1), (gv_hbm, heads + 1, 1)))
-        ]
+    ws = wrow // 2
+
+    def w_sub(direction, c, sub):
+        return pl.ds(pl.multiple_of(w_rows(direction, c) + sub * ws, ws), ws)
+
+    def rw_copy(direction, t, sub):
+        piece = arena.at[w_sub(direction, rs_chunk(direction, t), sub)]
+        return rcopy(piece, piece, rw_send.at[direction, t, sub], rw_recv.at[direction, t, sub], direction)
+
+    def rw_tick(direction, t, sub):
+        rows = w_sub(direction, rs_chunk(direction, t), sub)
+        rw_copy(direction, t - 1, sub).wait_recv()
+        arena[rows, :] = arena[rows, :] + part_w[direction, sub_rows(sub, ws), :]
+
+    def gw_copy(direction, t, sub):
+        piece = arena.at[w_sub(direction, ag_chunk(direction, t), sub)]
+        return rcopy(piece, piece, gw_send.at[direction, t, sub], gw_recv.at[direction, t, sub], direction)
 
     def extra_w():
         return extra_copy(arena.at[pl.ds(w_rows(first, rs_chunk(first, 0)), wrow)], extra_wb, 3)
@@ -482,36 +473,29 @@
     w_part(second, 0)
     pl.semaphore_wait(ready_sem, 2)
     arena[pl.ds(w_rows(second, rs_chunk(second, 0)), wrow), :] = part_w[second]
-    rw_copy(second, 0).start()
+    for sub in (0, 1):
+        rw_copy(second, 0, sub).start()
     w_part(first, 1)
-    rw_tick(first, 1)
-    rw_copy(first, 1).start()
+    for sub in (0, 1):
+        rw_tick(first, 1, sub)
+        rw_copy(first, 1, sub).start()
     w_part(first, 0)
     arena[pl.ds(w_rows(first, rs_chunk(first, 0)), wrow), :] = part_w[first]
     extra_w().start()
     w_part(second, 1)
     arena[pl.ds(w_rows(second, rs_chunk(second, 1)), wrow), :] = part_w[second]
-    rw_copy(second, 1).start()
+    for sub in (0, 1):
+        rw_copy(second, 1, sub).start()
     for direction in order:
         w_part(direction, 2)
 
-    def last_o():
-        at = pl.ds(pl.multiple_of(ag_chunk(second, n - 1) * mc, mc), mc)
-        rows = pl.ds(pl.multiple_of(second * eh, eh), eh)
-        return pltpu.make_async_copy(gift_ob, go_hbm.at[rows, at], out_o_sem.at[second, n - 1])
-
-    go_copy(first, n - 2).wait_recv()
-    go_out(first, n - 1).start()
-    gift_o().wait_recv()
-    last_o().start()
-    stage_copy(y_hbm, n - 2).wait()
-    stage_copy(y_hbm, n - 1).wait()
-
     def third_step(t, carry):
         wait_sends(rw_copy, t - 2)
+        for sub in (0, 1):
+            for direction in order:
+                rw_tick(direction, t, sub)
+                rw_copy(direction, t, sub).start()
         for direction in order:
-            rw_tick(direction, t)
-            rw_copy(direction, t).start()
             w_part(direction, t + 1)
         return carry
 
@@ -520,19 +504,17 @@
 
     def dx_piece(i):
         at = pl.ds(pl.multiple_of(i * mc, mc), mc)
-        stage[lax.rem(i, 2)] = dot_nt(dqkv[...], wqkv[at, :]).astype(BF16)
-        stage_copy(dx_hbm, i).start()
-
-    rw_tick(first, n - 1)
-    gw_copy(first, 0).start()
+        x[:, at] = dot_nt(dqkv[...], wqkv[at, :]).astype(BF16)
+
+    for sub in (0, 1):
+        rw_tick(first, n - 1, sub)
+        gw_copy(first, 0, sub).start()
     gift_w().start()
     extra_w().wait_recv()
     part_w[second] = part_w[second] + extra_wb[...]
-    rw_tick(second, n - 1)
-    gw_copy(second, 0).start()
-    for direction in order:
-        for copy in gw_out(direction, 0):
-            copy.start()
+    for sub in (0, 1):
+        rw_tick(second, n - 1, sub)
+        gw_copy(second, 0, sub).start()
     dx_piece(0)
     dx_piece(1)
 
@@ -541,44 +523,63 @@
         def _():
             wait_sends(rw_copy, n - 4 + t)
 
-        for direction in order:
-            gw_copy(direction, t - 1).wait_recv()
-            ag_send(gw_copy, direction, t)
-            for copy in gw_out(direction, t):
-                copy.start()
-        stage_copy(dx_hbm, t - 1).wait()
+        for sub in (0, 1):
+            for direction in order:
+                gw_copy(direction, t - 1, sub).wait_recv()
+                ag_send(gw_copy(direction, t, sub), direction, t)
         dx_piece(t + 1)
         return carry
 
     lax.fori_loop(1, n - 1, fourth_step, 0)
 
-    stage_copy(dx_hbm, n - 2).wait()
-    stage_copy(dx_hbm, n - 1).wait()
-
-    gw_copy(first, n - 2).wait_recv()
+    go_copy(first, n - 2).wait_recv()
+    gift_o().wait_recv()
+    for sub in (0, 1):
+        gw_copy(first, n - 2, sub).wait_recv()
     gift_w().wait_recv()
-    for copy in gw_out(first, n - 1) + gw_out(second, n - 1, gift_wb):
-        copy.start()
 
     def drain_all(t, c):
-        for copy in (go_copy, gw_copy):
-            copy(second, t).wait_send()
-
-            @pl.when(t < n - 2)
-            def _(copy=copy):
-                copy(first, t).wait_send()
-
-        for direction in (0, 1):
-            go_out(direction, t).wait()
-            for copy in gw_out(direction, t):
-                copy.wait()
+        def drain_gather(direction):
+            go_copy(direction, t).wait_send()
+            for sub in (0, 1):
+                gw_copy(direction, t, sub).wait_send()
+
+        drain_gather(second)
+
+        @pl.when(t < n - 2)
+        def _():
+            drain_gather(first)
+
         return c
 
     lax.fori_loop(0, n - 1, drain_all, 0)
-    for copy in [go_out(first, n - 1), last_o()] + gw_out(first, n - 1) + gw_out(second, n - 1, gift_wb):
-        copy.wait()
     for copy in (gift_o, gift_w):
         copy().wait_send()
+    last = ag_chunk(second, n - 1)
+    slot_o[second, last] = gift_ob[...]
+    arena[pl.ds(w_rows(second, last), wrow), :] = gift_wb[...]
+
+
+def store_kernel(n, heads, x, dy, slot_o, arena, y_hbm, dx_hbm, gq_hbm, gk_hbm, gv_hbm, go_hbm, sem_a, sem_b):
+    eh, mc = slot_o.shape[2:]
+    mh = mc // 2
+    wrow = mh * (heads + 2)
+    copies = [pltpu.make_async_copy(dy, y_hbm, sem_a.at[0]), pltpu.make_async_copy(x, dx_hbm, sem_a.at[1])]
+    for c in range(n):
+        for d in range(2):
+            dst = go_hbm.at[pl.ds(d * eh, eh), pl.ds(c * mc, mc)]
+            copies.append(pltpu.make_async_copy(slot_o.at[d, c], dst, sem_b.at[d, c, 0]))
+            row = (d * n + c) * wrow
+            start = c * mc + d * mh
+            for k, (out, skip, rows) in enumerate(((gq_hbm, 0, heads), (gk_hbm, heads, 1), (gv_hbm, heads + 1, 1))):
+                copies.append(pltpu.make_async_copy(
+                    arena.at[pl.ds(row + skip * mh, rows * mh)],
+                    out.at[pl.ds(start * rows, rows * mh)], sem_b.at[d, c, k + 1],
+                ))
+    for copy in copies:
+        copy.start()
+    for copy in copies:
+        copy.wait()
 
 
 def solution(mesh):
@@ -598,22 +599,20 @@
         wrow = mc // 2 * (heads + 2)
         dma = lambda *shape: pltpu.SemaphoreType.DMA(shape)
         ring = dma(2, n - 1)
-        outs = pl.pallas_call(
+        split_ring = dma(2, n - 1, 2)
+        arena_rows = max(4 * n * tok, 2 * n * wrow)
+        state = pl.pallas_call(
             functools.partial(layer_kernel, n, heads),
             name="attention_layer",
             out_shape=[
-                jax.ShapeDtypeStruct((tok, width), BF16),
-                jax.ShapeDtypeStruct((tok, width), BF16),
-                jax.ShapeDtypeStruct((width * heads, hd), F32),
-                jax.ShapeDtypeStruct((width, hd), F32),
-                jax.ShapeDtypeStruct((width, hd), F32),
-                jax.ShapeDtypeStruct((embed, width), F32),
+                pltpu.VMEM((tok, width), BF16),
+                pltpu.VMEM((tok, width), BF16),
+                pltpu.VMEM((2, n, embed // 2, mc), F32),
+                pltpu.VMEM((arena_rows, hd), F32),
             ],
             in_specs=[HBM] * 6,
-            out_specs=[HBM] * 6,
+            out_specs=[VMEM] * 4,
             scratch_shapes=[
-                pltpu.VMEM((tok, width), BF16),
-                pltpu.VMEM((tok, width), BF16),
                 pltpu.VMEM((width, embed + kvw), BF16),
                 pltpu.VMEM((embed, width), BF16),
                 pltpu.VMEM((n, tok, kvw), BF16),
@@ -628,12 +627,9 @@
                 pltpu.VMEM((2, 1, cols), F32),
                 pltpu.VMEM((2, 1, cols), F32),
                 pltpu.VMEM((tok, embed + kvw), BF16),
-                pltpu.VMEM((2, n, embed // 2, mc), F32),
                 pltpu.VMEM((2, embed // 2, mc), F32),
-                pltpu.VMEM((max(4 * n * tok, 2 * n * wrow), hd), F32),
                 pltpu.VMEM((2, wrow, hd), F32),
                 pltpu.VMEM((mc // 2, tok), BF16),
-                pltpu.VMEM((2, tok, mc), BF16),
                 pltpu.VMEM((embed // 2, mc), F32),
                 pltpu.VMEM((embed // 2, mc), F32),
                 pltpu.VMEM((tok, hd), F32),
@@ -641,18 +637,33 @@
                 pltpu.VMEM((wrow, hd), F32),
                 dma(6),
                 dma(2, n // 2), dma(2, n // 2),
-                ring, ring, ring, ring, ring, ring, ring, ring, ring, ring,
-                dma(5), dma(5), dma(2, n), dma(2, n, 3), dma(2),
+                split_ring, split_ring, ring, ring, ring, ring, split_ring, split_ring, split_ring, split_ring,
+                dma(5), dma(5),
                 pltpu.SemaphoreType.REGULAR,
             ],
             compiler_params=pltpu.CompilerParams(
-                collective_id=0, has_side_effects=True, vmem_limit_bytes=67_000_000
+                collective_id=0, has_side_effects=True, vmem_limit_bytes=30 * 2 ** 20
             ),
         )(
             hidden, grad_out, w_query.reshape(width, embed), w_key.reshape(width, hd), w_value.reshape(width, hd),
             w_out.reshape(embed, width),
         )
-        output, grad_hidden, gq, gk, gv, go = outs
+        output, grad_hidden, gq, gk, gv, go = pl.pallas_call(
+            functools.partial(store_kernel, n, heads),
+            name="store_results",
+            out_shape=[
+                jax.ShapeDtypeStruct((tok, width), BF16),
+                jax.ShapeDtypeStruct((tok, width), BF16),
+                jax.ShapeDtypeStruct((width * heads, hd), F32),
+                jax.ShapeDtypeStruct((width, hd), F32),
+                jax.ShapeDtypeStruct((width, hd), F32),
+                jax.ShapeDtypeStruct((embed, width), F32),
+            ],
+            in_specs=[VMEM] * 4,
+            out_specs=[HBM] * 6,
+            scratch_shapes=[dma(2), dma(2, n, 4)],
+            compiler_params=pltpu.CompilerParams(vmem_limit_bytes=2 ** 20),
+        )(*state)
         return (
             output,
             grad_hidden,

time: 342 us -> 333 us (0.974)
  local copies, waits for them, and re-layouts: 26.8 us -> 4.92 us
  Pallas kernels: 315 us -> 328 us
    unnamed x17 -> x1, local copies, waits for them, and re-layouts: 26.8 us -> 4.92 us
    pallas_call x0 -> x1, Pallas kernels: none -> 11 us  [device_layer(): pl.pallas_call(functools.partial(store_kernel, n, heads), name='store_res...]
where the time goes in v4:
time: 333 us
  Pallas kernels  328 us (98%)
  local copies, waits for them, and re-layouts  4.92 us (1%)
    pallas_call x1, Pallas kernels, device_layer(): pl.pallas_call(functools.partial(layer_kernel, n, heads), name='attention...  317 us
    pallas_call x1, Pallas kernels, device_layer(): pl.pallas_call(functools.partial(store_kernel, n, heads), name='store_res...  11 us

profile of v4, /device:TPU:21, one launch (start us, length us, event | category | flops | bytes accessed | tf_op | source)
XLA Modules:
  0.0 333.4 jit_solution(7343521543974007077)
XLA Ops:
  0.6 4.9 %copy.16 = bf16[512,8,4,128]{3,1,2,0:T(8,128)(2,1)} copy(bf16[512,8,4,128]{3,2,1,0:T(4,128)(2,1)} %bitcast.16) | data formatting | bytes 8388608
  5.6 316.7 %attention_layer.1 = (bf16[512,4096]{1,0:T(8,128)(2,1)S(1)}, bf16[512,4096]{1,0:T(8,128)(2,1)S(1)}, f32[2,16,256,256]{3,2,1,0:T(8,128)S(1)}, f32[32768,128]{1,0:T(8,128)S(1)}) custom-call(bf16[512,4096]{1,0:T(8,128)(2,1)} %x_hbm.1, bf16[512,4096]{1,0:T(8,128)(2,1)} %dy_hbm.1, bf16[4096,512]{1,0:T(8,128)(2,1)} %bitcast.15, bf16[4096,128]{1,0:T(8,128)(2,1)} %bitcast.18, ...), custom_call_target="tpu_custom_call" | custom-call | tf_op jit(solution)/shard_map/attention_layer/pallas_call | solution.py:604
  322.2 11.0 %store_results.1 = (bf16[512,4096]{1,0:T(8,128)(2,1)}, bf16[512,4096]{1,0:T(8,128)(2,1)}, f32[16384,128]{1,0:T(8,128)}, f32[4096,128]{1,0:T(8,128)}, f32[4096,128]{1,0:T(8,128)}, /*index=5*/f32[512,4096]{1,0:T(8,128)}) custom-call(bf16[512,4096]{1,0:T(8,128)(2,1)S(1)} %get-tuple-element.16.x, bf16[512,4096]{1,0:T(8,128)(2,1)S(1)} %get-tuple-element.17.dy, ...), custom_call_target="tpu_custom_call" | custom-call | tf_op jit(solution)/shard_map/store_results/pallas_call | solution.py:651

commit v5 on v4

--- a/solution.py
+++ b/solution.py
@@ -86,24 +86,29 @@
     kv[me] = dot(x[...], wqkv[:, embed:]).astype(BF16)
     pl.semaphore_wait(barrier, 2)
 
-    def kv_copy(direction, t):
-        c = ag_chunk(direction, t)
-        return rcopy(kv.at[c], kv.at[c], kv_send.at[direction, t], kv_recv.at[direction, t], direction)
+    def kv_copy(direction, t, sub):
+        piece = kv.at[ag_chunk(direction, t), pl.ds(pl.multiple_of(sub * half, half), half)]
+        return rcopy(piece, piece, kv_send.at[direction, t, sub], kv_recv.at[direction, t, sub], direction)
 
     def kv_steps(direction):
         return n // 2 + direction * (n - 1 - 2 * (n // 2))
 
-    def kv_tick(direction, t):
+    def kv_tick(direction, t, sub):
         @pl.when(t < kv_steps(direction))
         def _():
-            kv_copy(direction, t).wait_recv()
+            kv_copy(direction, t, sub).wait_recv()
 
             @pl.when(t + 1 < kv_steps(direction))
             def _():
-                kv_copy(direction, t + 1).start()
-
-    for direction in order:
-        kv_copy(direction, 0).start()
+                kv_copy(direction, t + 1, sub).start()
+
+    def kv_step(t, u):
+        kv_tick(first, t, u)
+        kv_tick(second, t, 1 - u)
+
+    for sub in (0, 1):
+        kv_copy(first, 0, sub).start()
+        kv_copy(second, 0, 1 - sub).start()
 
     def spread(block, rows_ref, cols_ref, h):
         for b in range(2):
@@ -126,7 +131,7 @@
     loads[3].wait()
     for g in range(embed // 256):
         project_q(g)
-        kv_tick(order[g % 2], g // 2)
+        kv_step(g // 2, g % 2)
     early = embed // 512
 
     m_state[...] = jnp.full(m_state.shape, -jnp.inf, F32)
@@ -162,7 +167,7 @@
 
     def forward_step(j, carry):
         direction = first + lax.rem(j, 2) * (second - first)
-        kv_tick(direction, j // 2 + early)
+        kv_step(j // 2 + early, lax.rem(j, 2))
         s = rs_chunk(direction, j // 2)
 
         def unit(u, c):
@@ -176,7 +181,8 @@
 
     for direction in (0, 1):
         def drain(t, c, direction=direction):
-            kv_copy(direction, t).wait_send()
+            for sub in (0, 1):
+                kv_copy(direction, t, sub).wait_send()
             return c
 
         lax.fori_loop(0, kv_steps(direction), drain, 0)
@@ -220,11 +226,11 @@
         ro_copy(direction, t - 1, sub).wait_recv()
         slot_o[direction, c, rows, :] = slot_o[direction, c, rows, :] + part_o[direction, rows, :]
 
-    def ro_step(t, sub):
-        for direction in order:
+    def ro_step(t, u):
+        for direction, sub in ((first, u), (second, 1 - u)):
             ro_tick(direction, t, sub)
             ro_copy(direction, t, sub).start()
-        for direction in order:
+        for direction, sub in ((first, u), (second, 1 - u)):
             wo_part(direction, t + 1, sub)
 
     def extra_copy(src, dst, k):
@@ -636,7 +642,7 @@
                 pltpu.VMEM((wrow, hd), F32),
                 pltpu.VMEM((wrow, hd), F32),
                 dma(6),
-                dma(2, n // 2), dma(2, n // 2),
+                dma(2, n // 2, 2), dma(2, n // 2, 2),
                 split_ring, split_ring, ring, ring, ring, ring, split_ring, split_ring, split_ring, split_ring,
                 dma(5), dma(5),
                 pltpu.SemaphoreType.REGULAR,

time: 333 us -> 370 us (1.11)
  Pallas kernels: 328 us -> 365 us
    pallas_call x1, Pallas kernels: 317 us -> 354 us  [device_layer(): pl.pallas_call(functools.partial(layer_kernel, n, heads), name='attention...]
where the time goes in v5:
time: 370 us
  Pallas kernels  365 us (99%)
  local copies, waits for them, and re-layouts  4.92 us (1%)
    pallas_call x1, Pallas kernels, device_layer(): pl.pallas_call(functools.partial(layer_kernel, n, heads), name='attention...  354 us
    pallas_call x1, Pallas kernels, device_layer(): pl.pallas_call(functools.partial(store_kernel, n, heads), name='store_res...  11 us

profile of v5, /device:TPU:21, one launch (start us, length us, event | category | flops | bytes accessed | tf_op | source)
XLA Modules:
  0.0 370.3 jit_solution(17624221920498836975)
XLA Ops:
  0.6 4.9 %copy.16 = bf16[512,8,4,128]{3,1,2,0:T(8,128)(2,1)} copy(bf16[512,8,4,128]{3,2,1,0:T(4,128)(2,1)} %bitcast.16) | data formatting | bytes 8388608
  5.6 353.6 %attention_layer.1 = (bf16[512,4096]{1,0:T(8,128)(2,1)S(1)}, bf16[512,4096]{1,0:T(8,128)(2,1)S(1)}, f32[2,16,256,256]{3,2,1,0:T(8,128)S(1)}, f32[32768,128]{1,0:T(8,128)S(1)}) custom-call(bf16[512,4096]{1,0:T(8,128)(2,1)} %x_hbm.1, bf16[512,4096]{1,0:T(8,128)(2,1)} %dy_hbm.1, bf16[4096,512]{1,0:T(8,128)(2,1)} %bitcast.15, bf16[4096,128]{1,0:T(8,128)(2,1)} %bitcast.18, ...), custom_call_target="tpu_custom_call" | custom-call | tf_op jit(solution)/shard_map/attention_layer/pallas_call | solution.py:610
  359.1 11.0 %store_results.1 = (bf16[512,4096]{1,0:T(8,128)(2,1)}, bf16[512,4096]{1,0:T(8,128)(2,1)}, f32[16384,128]{1,0:T(8,128)}, f32[4096,128]{1,0:T(8,128)}, f32[4096,128]{1,0:T(8,128)}, /*index=5*/f32[512,4096]{1,0:T(8,128)}) custom-call(bf16[512,4096]{1,0:T(8,128)(2,1)S(1)} %get-tuple-element.16.x, bf16[512,4096]{1,0:T(8,128)(2,1)S(1)} %get-tuple-element.17.dy, ...), custom_call_target="tpu_custom_call" | custom-call | tf_op jit(solution)/shard_map/store_results/pallas_call | solution.py:657

commit v6 on v4

--- a/solution.py
+++ b/solution.py
@@ -220,12 +220,16 @@
         ro_copy(direction, t - 1, sub).wait_recv()
         slot_o[direction, c, rows, :] = slot_o[direction, c, rows, :] + part_o[direction, rows, :]
 
-    def ro_step(t, sub):
-        for direction in order:
-            ro_tick(direction, t, sub)
-            ro_copy(direction, t, sub).start()
-        for direction in order:
-            wo_part(direction, t + 1, sub)
+    def ro_send_on(direction, t, sub):
+        ro_tick(direction, t, sub)
+        ro_copy(direction, t, sub).start()
+
+    def ro_step(t, u):
+        pair = ((first, t, u), (second, t - 1 + u, 1 - u))
+        for direction, at, sub in pair:
+            ro_send_on(direction, at, sub)
+        for direction, at, sub in pair:
+            wo_part(direction, at + 1, sub)
 
     def extra_copy(src, dst, k):
         return rcopy(src, dst, extra_send.at[k], extra_recv.at[k], second)
@@ -260,8 +264,11 @@
     loads[5].wait()
     for g in range(embed // 256):
         project_do(g)
-        if g < 2:
-            ro_step(2, g)
+        if g == 0:
+            ro_send_on(first, 2, 0)
+            wo_part(first, 3, 0)
+        if g == 1:
+            ro_step(2, 1)
     for b in range(2):
         for h in range(heads):
             lanes = slice(h * half, (h + 1) * half)
@@ -319,6 +326,11 @@
             @pl.when(t < n - 1)
             def _():
                 ro_step(t, u)
+
+            @pl.when(jnp.logical_and(t == n - 1, u == 0))
+            def _():
+                ro_send_on(second, n - 2, 1)
+                wo_part(second, n - 1, 1)
 
             qb, kb = unit_blocks(s, u)
             backward_unit(s, qb, kb, False, True)

time: 333 us -> 324 us (0.973)
  Pallas kernels: 328 us -> 318 us
    pallas_call x1, Pallas kernels: 317 us -> 307 us  [device_layer(): pl.pallas_call(functools.partial(layer_kernel, n, heads), name='attention...]
where the time goes in v6:
time: 324 us
  Pallas kernels  318 us (98%)
  local copies, waits for them, and re-layouts  4.92 us (2%)
    pallas_call x1, Pallas kernels, device_layer(): pl.pallas_call(functools.partial(layer_kernel, n, heads), name='attention...  307 us
    pallas_call x1, Pallas kernels, device_layer(): pl.pallas_call(functools.partial(store_kernel, n, heads), name='store_res...  11 us

profile of v6, /device:TPU:21, one launch (start us, length us, event | category | flops | bytes accessed | tf_op | source)
XLA Modules:
  0.0 324.1 jit_solution(12501211414697630552)
XLA Ops:
  0.6 4.9 %copy.16 = bf16[512,8,4,128]{3,1,2,0:T(8,128)(2,1)} copy(bf16[512,8,4,128]{3,2,1,0:T(4,128)(2,1)} %bitcast.16) | data formatting | bytes 8388608
  5.6 307.4 %attention_layer.1 = (bf16[512,4096]{1,0:T(8,128)(2,1)S(1)}, bf16[512,4096]{1,0:T(8,128)(2,1)S(1)}, f32[2,16,256,256]{3,2,1,0:T(8,128)S(1)}, f32[32768,128]{1,0:T(8,128)S(1)}) custom-call(bf16[512,4096]{1,0:T(8,128)(2,1)} %x_hbm.1, bf16[512,4096]{1,0:T(8,128)(2,1)} %dy_hbm.1, bf16[4096,512]{1,0:T(8,128)(2,1)} %bitcast.15, bf16[4096,128]{1,0:T(8,128)(2,1)} %bitcast.18, ...), custom_call_target="tpu_custom_call" | custom-call | tf_op jit(solution)/shard_map/attention_layer/pallas_call | solution.py:616
  313.0 11.0 %store_results.1 = (bf16[512,4096]{1,0:T(8,128)(2,1)}, bf16[512,4096]{1,0:T(8,128)(2,1)}, f32[16384,128]{1,0:T(8,128)}, f32[4096,128]{1,0:T(8,128)}, f32[4096,128]{1,0:T(8,128)}, /*index=5*/f32[512,4096]{1,0:T(8,128)}) custom-call(bf16[512,4096]{1,0:T(8,128)(2,1)S(1)} %get-tuple-element.16.x, bf16[512,4096]{1,0:T(8,128)(2,1)S(1)} %get-tuple-element.17.dy, ...), custom_call_target="tpu_custom_call" | custom-call | tf_op jit(solution)/shard_map/store_results/pallas_call | solution.py:663
